TPU v7x, 32 devices: a whole 2x2x4 slice. The times are simulated.
32 devices in a mesh: dp: 8 (over z, core), mp: 4 (over y, x).
Axes of the slice: x: 2, y: 2, z: 4, core: 2. Of those that a mesh axis runs over, the one named last changes fastest.
Arguments:
- hidden_states: bfloat16 [32, 640, 1280], P(('dp', 'mp')), may hold values from -6 to 6
- ln_attn_gain: float32 [1280], replicated, may hold values from 0.1 to 1.9
- w_qkv: bfloat16 [1280, 16, 192], P(None, 'mp'), may hold values from -0.15625 to 0.15625
- output_weight: bfloat16 [64, 16, 1280], P(None, 'mp'), may hold values from -0.75 to 0.75
- ln_final_gain: float32 [1280], replicated, may hold values from 0.1 to 1.9
- dense_weight: bfloat16 [1280, 1280], replicated, may hold values from -0.15625 to 0.15625
- decoder_weight: bfloat16 [1280, 33], replicated, may hold values from -0.5390625 to 0.5390625
- decoder_bias: float32 [33], replicated, may hold values from -4 to 4
- seq_tokens: int32 [24, 640], replicated, may hold values from 4 to 23
- seq_lengths: int32 [24], replicated, may hold values from 128 to 640
- copy_sequence: int32 [32], replicated, may hold values from 0 to 23
- mask_code: int32 [32, 64], replicated, may hold values from 0 to 1048575
- copy_owner: int32 [32], replicated, may hold values from 0 to 31, each once
Outputs:
- pll: float32 [32, 64], P('dp', 'mp')
Inputs may be any that keep to these rules, and one draw needn't show every extreme that they name: `seq_tokens`: amino-acid token ids. `copy_owner`: every row of pll is named by exactly one copy.
All inputs are finite; a program needn't handle non-finite values.
Results may differ from a plain program's by a relative error of at most 0.0038.
Values may be sent and summed in bfloat16 or wider, within the bound.
A program may use at most 128 MiB of HBM per device.

v0:
```python
import functools

import jax
import jax.numpy as jnp
import numpy as np
from jax import lax
from jax.experimental import pallas as pl
from jax.experimental.pallas import tpu as pltpu
from jax.sharding import PartitionSpec as P

epsilon = 1e-05
MESH = pl.DeviceIdType.MESH
f32 = jnp.float32
bf16 = jnp.bfloat16
LANES = 128


def layer_norm(inputs):
    average = jnp.mean(inputs, axis=-1, keepdims=True)
    centred = inputs - average
    variance = jnp.mean(centred * centred, axis=-1, keepdims=True)
    return centred * lax.rsqrt(variance + epsilon)


def rotary_tables(seq_span, head_size):
    half = head_size // 2
    frequency = (1.0 / 10000.0 ** (np.arange(half, dtype=np.float32) * (2.0 / head_size))).astype(
        np.float32
    )
    angles = np.arange(seq_span, dtype=np.float32)[:, None] * frequency[None, :]
    cosine, sine = np.cos(angles), np.sin(angles)
    times = LANES // head_size
    return (
        np.tile(np.concatenate([cosine, cosine], axis=1), (1, times)).astype(np.float32),
        np.tile(np.concatenate([-sine, sine], axis=1), (1, times)).astype(np.float32),
    )


def flip(index, mask):
    bit = 1
    out = index
    while bit <= mask:
        if mask & bit:
            out = out + bit * (1 - 2 * ((index // bit) % 2))
        bit *= 2
    return out


def kernel(
    sizes,
    sequence_ref,
    lengths_ref,
    codes_ref,
    tokens_ref,
    owner_ref,
    gain_ref,
    final_gain_ref,
    decoder_ref,
    bias_ref,
    hidden_hbm,
    weight_hbm,
    out_weight_hbm,
    dense_hbm,
    cos_hbm,
    sin_hbm,
    out_ref,
    hidden,
    normed,
    wbuf,
    obuf,
    dense,
    cos,
    sin,
    pbuf,
    context,
    mixed,
    scores,
    local_sem,
    direct_sem,
    relay_sem,
    exchange_sem,
    share_sem,
    arrive_sem,
    shared_sem,
    score_send_sem,
    score_sem,
):
    n_dp, n_mp, head_size, heads_in_chunk, chunks = sizes
    devices = n_dp * n_mp
    dp = lax.axis_index("dp")
    mp = lax.axis_index("mp")
    core = dp % 2
    partner = dp + 1 - 2 * core
    me = dp * n_mp + mp
    seq_span, feature = hidden.shape
    masks = codes_ref.shape[1]
    chunk_heads = heads_in_chunk * head_size
    out_rows = obuf.shape[1]
    piece_rows = out_rows // 4

    def local(index, source, target):
        copy = pltpu.make_async_copy(source, target, local_sem.at[index])
        copy.start()
        return copy

    weight_copy = local(1, weight_hbm, wbuf.at[0])
    hidden_copy = local(0, hidden_hbm, hidden)

    barrier = pltpu.get_barrier_semaphore()

    def greet(step, carry):
        other = (me + step) % devices
        pl.semaphore_signal(
            barrier, inc=1, device_id=(other // n_mp, other % n_mp), device_id_type=MESH
        )
        return carry

    lax.fori_loop(1, devices, greet, 0)

    parity = (dp // 2) % 2
    above = dp + 2 - 4 * parity
    part_rows = wbuf.shape[2] // 4

    def part(chunk, odd):
        return 2 * chunk + odd

    def place(relation, item, half):
        if item < 2 * chunks:
            chunk, odd = divmod(item, 2)
            which = 1 - parity if odd else parity
            start = (2 * half + which) * part_rows
            return wbuf.at[relation, chunk, pl.ds(pl.multiple_of(start, 16), part_rows), :]
        start = (2 * half + item - 2 * chunks) * piece_rows
        return obuf.at[relation, pl.ds(pl.multiple_of(start, 16), piece_rows), :]

    def view(relation, item):
        return place(relation, item, core)

    def partner_view(relation, item):
        return place(relation, item, 1 - core)

    sent = []

    def to_group(target, source_relation, relation, item, semaphore):
        copy = pltpu.make_async_remote_copy(
            src_ref=view(source_relation, item),
            dst_ref=view(relation, item),
            send_sem=semaphore,
            recv_sem=arrive_sem.at[relation, item],
            device_id=(dp, flip(mp, target)),
            device_id_type=MESH,
        )
        copy.start()
        sent.append(copy)

    def direct(target, item):
        to_group(target, 0, target, item, direct_sem.at[target, item])

    def relay(target, source_relation, item):
        to_group(target, source_relation, source_relation ^ target, item, relay_sem.at[item])

    def exchange(relation, chunk):
        copy = pltpu.make_async_remote_copy(
            src_ref=view(relation, part(chunk, 0)),
            dst_ref=view(relation, part(chunk, 0)),
            send_sem=exchange_sem.at[relation, chunk],
            recv_sem=arrive_sem.at[relation, part(chunk, 1)],
            device_id=(above, mp),
            device_id_type=MESH,
        )
        copy.start()
        sent.append(copy)

    def arrived(relation, item):
        landing = view(relation, item)
        pltpu.make_async_copy(landing, landing, arrive_sem.at[relation, item]).wait()

    def share(relation, item):
        copy = pltpu.make_async_remote_copy(
            src_ref=view(relation, item),
            dst_ref=view(relation, item),
            send_sem=share_sem.at[relation, item],
            recv_sem=shared_sem.at[relation, item],
            device_id=(partner, mp),
            device_id_type=MESH,
        )
        copy.start()
        sent.append(copy)

    def was_shared(relation, item):
        landing = partner_view(relation, item)
        pltpu.make_async_copy(landing, landing, shared_sem.at[relation, item]).wait()

    sequence = sequence_ref[me]
    length = lengths_ref[sequence].astype(f32)
    codes = codes_ref[pl.ds(me, 1), :].astype(f32)
    quotient = jnp.floor(codes / length)
    row_positions = codes - quotient * length
    row_positions = jnp.where(row_positions < 0.0, row_positions + length, row_positions)
    row_positions = jnp.where(row_positions >= length, row_positions - length, row_positions)
    eye = lax.broadcasted_iota(jnp.int32, (masks, masks), 0) == lax.broadcasted_iota(
        jnp.int32, (masks, masks), 1
    )
    positions = jnp.sum(jnp.where(eye, row_positions, 0.0), axis=1, keepdims=True)
    places = lax.broadcasted_iota(jnp.int32, (masks, seq_span), 1).astype(f32)
    chosen = places == positions
    onehot = jnp.where(chosen, 1.0, 0.0)
    onehot_bf = onehot.astype(bf16)
    tokens = tokens_ref[pl.ds(sequence, 1), :].astype(f32)
    targets = jnp.sum(jnp.where(chosen, tokens, 0.0), axis=1, keepdims=True)
    alive = lax.broadcasted_iota(jnp.int32, (1, seq_span), 1).astype(f32) < length

    weight_copy.wait()
    pl.semaphore_wait(barrier, devices - 1)
    items = 2 * chunks + 2
    routed = n_mp == 4 and chunks == 2 and n_dp % 4 == 0
    if routed:
        direct(1, part(1, 0))
        direct(2, part(0, 0))
        direct(1, part(0, 0))
        direct(2, part(1, 0))
    cos_copy = local(3, cos_hbm, cos)
    sin_copy = local(4, sin_hbm, sin)
    out_weight_copy = local(2, out_weight_hbm, obuf.at[0])
    dense_copy = local(5, dense_hbm, dense)
    if not routed:
        out_weight_copy.wait()
        for item in range(items):
            for target in range(1, n_mp):
                direct(target, item)

    hidden_copy.wait()
    tile = 128 if seq_span % 128 == 0 else 8

    def norm_rows(step, carry):
        rows = pl.ds(pl.multiple_of(step * tile, tile), tile)
        normed[rows, :] = (layer_norm(hidden[rows, :].astype(f32)) * gain_ref[...].reshape(1, feature)).astype(bf16)
        return carry

    lax.fori_loop(0, seq_span // tile, norm_rows, 0)
    masked_rows = jnp.dot(onehot_bf, normed[...], preferred_element_type=f32).astype(bf16)
    own_rows = jnp.dot(onehot_bf, hidden[...], preferred_element_type=f32)
    mixed[...] = own_rows
    cos_copy.wait()
    sin_copy.wait()
    exact = dict(preferred_element_type=f32, precision=lax.Precision.HIGHEST)
    query_cos = jnp.dot(onehot, cos[...], **exact)
    query_sin = jnp.dot(onehot, sin[...], **exact)
    lane = lax.broadcasted_iota(jnp.int32, (1, LANES), 1)
    first = lane % head_size < head_size // 2

    def rotate(inputs, cosine, sine):
        turned = jnp.where(
            first,
            pltpu.roll(inputs, LANES - head_size // 2, 1),
            pltpu.roll(inputs, head_size // 2, 1),
        )
        return inputs * cosine + turned * sine

    transposed = (((1,), (1,)), ((), ()))
    low = lane < head_size
    span = seq_span // 2 if seq_span % 32 == 0 else seq_span
    head_rows = 3 * head_size

    def attend(relation, chunk):
        weights = wbuf.at[relation, chunk]
        pairs = [
            weights[head * head_rows + head_size : (head + 1) * head_rows, :]
            for head in range(heads_in_chunk)
        ]
        pair_weights = pairs[0] if heads_in_chunk == 1 else jnp.concatenate(pairs, axis=0)

        def project(step, carry):
            rows = pl.ds(pl.multiple_of(step * span, 16), span)
            made = lax.dot_general(
                normed[rows, :], pair_weights, transposed, preferred_element_type=f32
            )
            for head in range(heads_in_chunk):
                block = made[:, head * LANES : (head + 1) * LANES]
                block = jnp.where(low, rotate(block, cos[rows, :], sin[rows, :]), block)
                pbuf[rows, head * LANES : (head + 1) * LANES] = block.astype(bf16)
            return carry

        lax.fori_loop(0, seq_span // span, project, 0)
        if heads_in_chunk == 1:
            query_weights = weights[: 2 * head_size, :]
        else:
            query_weights = jnp.concatenate(
                [weights[:head_size, :], weights[head_rows : head_rows + head_size, :]], axis=0
            )
        made = lax.dot_general(masked_rows, query_weights, transposed, preferred_element_type=f32)
        turned = rotate(made * head_size ** (-0.5), query_cos, query_sin)
        vectors = []
        for head in range(heads_in_chunk):
            query = turned if head == 0 else pltpu.roll(turned, head_size, 1)
            query = jnp.where(low, query, 0.0).astype(bf16)
            block = pbuf[:, head * LANES : (head + 1) * LANES]
            logits = lax.dot_general(query, block, transposed, preferred_element_type=f32)
            logits = jnp.where(alive, logits, -1e30)
            weight = jnp.exp(logits - jnp.max(logits, axis=-1, keepdims=True))
            probs = (weight / jnp.sum(weight, axis=-1, keepdims=True)).astype(bf16)
            vectors.append(jnp.dot(probs, block, preferred_element_type=f32))
        total = pltpu.roll(vectors[0], head_size, 1)
        if heads_in_chunk > 1:
            total = jnp.where(low, total, vectors[1])
        context[relation, chunk] = total[:, :chunk_heads].astype(bf16)

    def mix(relation):
        for chunk in range(chunks):
            rows = slice(chunk * chunk_heads, (chunk + 1) * chunk_heads)
            mixed[...] += jnp.dot(
                context[relation, chunk], obuf[relation, rows, :], preferred_element_type=f32
            )

    def fetch(*pairs):
        for pair in pairs:
            arrived(*pair)
            share(*pair)

    def attend_shared(relation, chunk):
        was_shared(relation, part(chunk, 0))
        was_shared(relation, part(chunk, 1))
        attend(relation, chunk)

    attend(0, 0)
    if routed:
        first_piece, second_piece = 2 * chunks, 2 * chunks + 1
        arrived(1, part(1, 0))
        relay(2, 1, part(1, 0))
        exchange(1, 1)
        share(1, part(1, 0))
        arrived(2, part(0, 0))
        relay(1, 2, part(0, 0))
        exchange(2, 0)
        share(2, part(0, 0))
        direct(1, part(0, 1))
        direct(2, part(1, 1))
        out_weight_copy.wait()
        direct(1, first_piece)
        direct(2, second_piece)
        direct(1, second_piece)
        direct(2, first_piece)
    for chunk in range(1, chunks):
        attend(0, chunk)
    mix(0)
    if routed:
        fetch((1, part(0, 0)), (2, part(1, 0)), (1, part(1, 1)))
        arrived(3, part(0, 0))
        exchange(3, 0)
        share(3, part(0, 0))
        arrived(3, part(1, 0))
        exchange(3, 1)
        share(3, part(1, 0))
        fetch((2, part(0, 1)))
        attend_shared(1, 1)
        attend_shared(2, 0)
        fetch((1, part(0, 1)), (2, part(1, 1)), (3, part(0, 1)))
        attend_shared(1, 0)
        arrived(1, first_piece)
        relay(2, 1, first_piece)
        share(1, first_piece)
        arrived(2, second_piece)
        relay(1, 2, second_piece)
        share(2, second_piece)
        attend_shared(2, 1)
        fetch((3, part(1, 1)))
        attend_shared(3, 0)
        fetch((1, second_piece), (2, first_piece))
        attend_shared(3, 1)
        for relation in (1, 2):
            was_shared(relation, first_piece)
            was_shared(relation, second_piece)
            mix(relation)
        fetch((3, first_piece), (3, second_piece))
        was_shared(3, first_piece)
        was_shared(3, second_piece)
        mix(3)
    else:
        for relation in range(1, n_mp):
            fetch(*[(relation, item) for item in range(items)])
        for relation in range(1, n_mp):
            for item in range(items):
                was_shared(relation, item)
            for chunk in range(chunks):
                attend(relation, chunk)
            mix(relation)

    normed_final = (layer_norm(mixed[...]) * final_gain_ref[...].reshape(1, feature)).astype(bf16)
    dense_copy.wait()
    dense_out = jnp.dot(normed_final, dense[...], preferred_element_type=f32)
    headed = layer_norm(0.5 * dense_out * (1.0 + lax.erf(dense_out * 0.5**0.5))).astype(bf16)
    logits = lax.dot_general(headed, decoder_ref[...], transposed, preferred_element_type=f32) + bias_ref[...]
    largest = jnp.max(logits, axis=-1, keepdims=True)
    scale = jnp.log(jnp.sum(jnp.exp(logits - largest), axis=-1, keepdims=True)) + largest
    vocabulary = lax.broadcasted_iota(jnp.int32, logits.shape, 1).astype(f32)
    picked = jnp.sum(jnp.where(vocabulary == targets, logits - scale, 0.0), axis=1, keepdims=True)
    row = jnp.sum(jnp.where(eye, picked, 0.0), axis=0, keepdims=True)
    padded = jnp.pad(row, ((0, 0), (0, LANES - masks)))
    scores[me] = jnp.broadcast_to(padded, scores.shape[1:])

    def score_copy(step):
        other = (me + step) % devices
        return pltpu.make_async_remote_copy(
            src_ref=scores.at[me, pl.ds(0, 1), :],
            dst_ref=scores.at[me, pl.ds(0, 1), :],
            send_sem=score_send_sem.at[step],
            recv_sem=score_sem.at[me],
            device_id=(other // n_mp, other % n_mp),
            device_id_type=MESH,
        )

    def send_scores(step, carry):
        score_copy(step).start()
        return carry

    lax.fori_loop(1, devices, send_scores, 0)
    for copy in sent:
        copy.wait_send()

    def wait_scores(step, carry):
        source = (me + step) % devices
        landing = scores.at[source, pl.ds(0, 1), :]
        pltpu.make_async_copy(landing, landing, score_sem.at[source]).wait()
        return carry

    lax.fori_loop(1, devices, wait_scores, 0)

    def wait_sends(step, carry):
        score_copy(step).wait_send()
        return carry

    lax.fori_loop(1, devices, wait_sends, 0)
    group = out_ref.shape[0]
    wanted = dp * group + lax.broadcasted_iota(jnp.int32, (group, owner_ref.shape[1]), 0)
    select = jnp.where(owner_ref[...] == wanted, 1.0, 0.0)
    out_ref[...] = jnp.dot(select, scores[:, 0, :], **exact)


def on_device(
    shape,
    hidden_states,
    ln_attn_gain,
    w_qkv,
    output_weight,
    ln_final_gain,
    dense_weight,
    decoder_weight,
    decoder_bias,
    seq_tokens,
    seq_lengths,
    copy_sequence,
    mask_code,
    copy_owner,
):
    n_dp, n_mp = shape
    devices = n_dp * n_mp
    lane_copies, seq_span, feature = hidden_states.shape
    head_size, heads, _ = output_weight.shape
    copies, masks = mask_code.shape
    assert lane_copies == 1 and copies == devices and n_dp % 2 == 0
    assert 2 * head_size == LANES and masks <= LANES
    in_chunk = 2 if heads % 2 == 0 else 1
    chunks = heads // in_chunk
    width = in_chunk * 3 * head_size
    weight = jnp.transpose(w_qkv.reshape(feature, chunks, width), (1, 2, 0))
    out_weight = jnp.swapaxes(output_weight, 0, 1).reshape(heads * head_size, feature)
    cosine, sine = rotary_tables(seq_span, head_size)
    group = copies // n_dp
    items = 2 * chunks + 2
    dma = pltpu.SemaphoreType.DMA
    vmem = pl.BlockSpec(memory_space=pltpu.VMEM)
    smem = pl.BlockSpec(memory_space=pltpu.SMEM)
    anywhere = pl.BlockSpec(memory_space=pl.ANY)
    rows = pl.pallas_call(
        functools.partial(kernel, (n_dp, n_mp, head_size, in_chunk, chunks)),
        name="score_copies",
        out_shape=jax.ShapeDtypeStruct((group, LANES), f32),
        in_specs=[smem] * 2 + [vmem] * 7 + [anywhere] * 6,
        out_specs=vmem,
        scratch_shapes=[
            pltpu.VMEM((seq_span, feature), bf16),
            pltpu.VMEM((seq_span, feature), bf16),
            pltpu.VMEM((n_mp, chunks, width, feature), bf16),
            pltpu.VMEM((n_mp, heads * head_size, feature), bf16),
            pltpu.VMEM((feature, feature), bf16),
            pltpu.VMEM((seq_span, LANES), f32),
            pltpu.VMEM((seq_span, LANES), f32),
            pltpu.VMEM((seq_span, in_chunk * LANES), bf16),
            pltpu.VMEM((n_mp, chunks, masks, in_chunk * head_size), bf16),
            pltpu.VMEM((masks, feature), f32),
            pltpu.VMEM((devices, 8, LANES), f32),
            dma((6,)),
            dma((n_mp, items)),
            dma((items,)),
            dma((n_mp, chunks)),
            dma((n_mp, items)),
            dma((n_mp, items)),
            dma((n_mp, items)),
            dma((devices,)),
            dma((devices,)),
        ],
        compiler_params=pltpu.CompilerParams(collective_id=0, has_side_effects=True),
    )(
        copy_sequence,
        seq_lengths,
        mask_code,
        seq_tokens,
        copy_owner.reshape(1, -1),
        ln_attn_gain,
        ln_final_gain,
        decoder_weight.T,
        decoder_bias.reshape(1, -1),
        hidden_states.reshape(seq_span, feature),
        weight,
        out_weight,
        dense_weight,
        jnp.asarray(cosine),
        jnp.asarray(sine),
    )
    own = masks // n_mp
    return lax.dynamic_slice_in_dim(rows, lax.axis_index("mp") * own, own, 1)


def solution(mesh):
    placed = (
        P(("dp", "mp"), None, None),
        P(),
        P(None, "mp", None),
        P(None, "mp", None),
        P(),
        P(),
        P(),
        P(),
        P(),
        P(),
        P(),
        P(),
        P(),
    )
    shape = (mesh.shape["dp"], mesh.shape["mp"])
    return jax.shard_map(
        functools.partial(on_device, shape),
        mesh=mesh,
        in_specs=placed,
        out_specs=P("dp", "mp"),
        check_vma=False,
    )
```

profile of v0, /device:TPU:0, one launch (start us, length us, event | category | flops | bytes accessed | tf_op | source)
XLA Modules:
  0.0 56.8 jit_solution(14298764764992810529)
XLA Ops:
  0.0 2.0 %copy.16 = bf16[4,64,1280]{2,1,0:T(8,128)(2,1)} copy(bf16[4,64,1280]{2,0,1:T(4,128)(2,1)} %bitcast.12) | data formatting | bytes 1310720 | tf_op jit(solution)/shard_map/transpose | solution.py:466
  2.0 53.5 %score_copies.1 = f32[4,128]{1,0:T(4,128)} custom-call(s32[32]{0:T(128)} %sequence_ref.1, s32[24]{0:T(128)} %lengths_ref.1, s32[32,64]{1,0:T(8,128)} %codes_ref.1, s32[24,640]{1,0:T(8,128)} %tokens_ref.1, s32[1,32]{1,0:T(1,128)} %bitcast.14, f32[1280]{0:T(1024)} %gain_ref.1, f32[1280]{0:T(1024)} %final_gain_ref.1, bf16[33,1280]{1,0:T(8,128)(2,1)} %bitcast.13, ...), custom_call_target="tpu_custom_call" | custom-call | tf_op jit(solution)/shard_map/score_copies/pallas_call | solution.py:474
  55.5 1.3 %constant_dynamic-slice_fusion = f32[4,16]{1,0:T(4,128)} fusion(f32[4,128]{1,0:T(4,128)} %score_copies.1, s32[]{:T(128)S(6)} %select_n.3), kind=kLoop, calls=%fused_computation | loop fusion | bytes 516 | tf_op jit(solution)/shard_map/dynamic_slice | solution.py:521
where the time goes:
time: 57 us; the launch traced here: 56.8 us
  Pallas kernels  53.5 us (94%)
  local copies, waits for them, and re-layouts  3.27 us (6%)
    pallas_call x1, Pallas kernels, on_device(): pl.pallas_call(functools.partial(kernel, (n_dp, n_mp, head_size, in_chunk...  53.5 us
    transpose x1, local copies, waits for them, and re-layouts, on_device(): jnp.swapaxes(output_weight, 0, 1).reshape(heads * head_size, feature)  1.99 us
    dynamic_slice x1, local copies, waits for them, and re-layouts, on_device(): return lax.dynamic_slice_in_dim(rows, lax.axis_index('mp') * own, own, 1)  1.29 us

commit v1 on v0

--- a/solution.py
+++ b/solution.py
@@ -436,6 +436,505 @@
     out_ref[...] = jnp.dot(select, scores[:, 0, :], **exact)
 
 
+KF, VF, QF, OF, KS, VS, QS, OS = range(8)
+
+
+def split_kernel(
+    sizes,
+    sequence_ref,
+    lengths_ref,
+    codes_ref,
+    tokens_ref,
+    owner_ref,
+    gain_ref,
+    final_gain_ref,
+    decoder_ref,
+    bias_ref,
+    hidden_hbm,
+    weight_hbm,
+    out_weight_hbm,
+    dense_hbm,
+    cos_hbm,
+    sin_hbm,
+    split_hbm,
+    out_ref,
+    hidden,
+    normed,
+    rows_buf,
+    wbuf,
+    obuf,
+    dense,
+    cos,
+    sin,
+    split,
+    pbuf,
+    context,
+    mixed,
+    inbox,
+    scores,
+    local_sem,
+    send_sem,
+    arrive_sem,
+    norm_send_sem,
+    norm_sem,
+    swap_send_sem,
+    swap_sem,
+    score_send_sem,
+    score_sem,
+    token_sem,
+):
+    n_dp, n_mp, head_size = sizes
+    devices = n_dp * n_mp
+    layers = n_dp // 2
+    dp = lax.axis_index("dp")
+    mp = lax.axis_index("mp")
+    core = dp % 2
+    layer = dp // 2
+    partner = dp + 1 - 2 * core
+    me = dp * n_mp + mp
+    mate = partner * n_mp + mp
+    parity = layer % 2
+    above = dp + 2 - 4 * parity
+    seq_span, feature = hidden.shape
+    masks = codes_ref.shape[1]
+    head_rows = 3 * head_size
+
+    barrier = pltpu.get_barrier_semaphore()
+
+    def signal(semaphore, where):
+        pl.semaphore_signal(semaphore, inc=1, device_id=where, device_id_type=MESH)
+
+    signal(barrier, (partner, mp))
+    signal(barrier, (dp, flip(mp, 1)))
+    signal(barrier, (dp, flip(mp, 2)))
+
+    @pl.when(layer > 0)
+    def _():
+        signal(barrier, (dp - 2, mp))
+
+    @pl.when(layer < layers - 1)
+    def _():
+        signal(barrier, (dp + 2, mp))
+
+    def local(index, source, target):
+        copy = pltpu.make_async_copy(source, target, local_sem.at[index])
+        copy.start()
+        return copy
+
+    weight_copy = local(1, weight_hbm.at[core], wbuf.at[0])
+    hidden_copy = local(0, hidden_hbm, hidden)
+    cos_copy = local(3, cos_hbm, cos)
+    sin_copy = local(4, sin_hbm, sin)
+    split_copy = local(6, split_hbm, split)
+    out_weight_copy = local(2, out_weight_hbm.at[pl.ds(pl.multiple_of(core * 2 * head_size, 128), 2 * head_size), :], obuf.at[0])
+    dense_copy = local(5, dense_hbm, dense)
+
+    def head_of(item):
+        return parity if item < KS else 1 - parity
+
+    def view(relation, item):
+        head, kind = head_of(item), item % 4
+        if kind == OF:
+            return obuf.at[relation, pl.ds(pl.multiple_of(head * head_size, head_size), head_size), :]
+        start = head * head_rows + (head_size, 2 * head_size, 0)[kind]
+        return wbuf.at[relation, pl.ds(pl.multiple_of(start, head_size), head_size), :]
+
+    sent = []
+
+    def send(source_relation, item, relation, landing, where):
+        copy = pltpu.make_async_remote_copy(
+            src_ref=view(source_relation, item),
+            dst_ref=view(source_relation ^ relation if relation != 4 else source_relation, item),
+            send_sem=send_sem.at[len(sent)],
+            recv_sem=arrive_sem.at[source_relation ^ relation if relation != 4 else source_relation, landing],
+            device_id=where,
+            device_id_type=MESH,
+        )
+        copy.start()
+        sent.append(copy)
+
+    def to_x(item, source_relation=0):
+        send(source_relation, item, 1, item, (dp, flip(mp, 1)))
+
+    def to_y(item, source_relation=0):
+        send(source_relation, item, 2, item, (dp, flip(mp, 2)))
+
+    def to_z(item, source_relation):
+        send(source_relation, item, 4, item + 4, (above, mp))
+
+    def arrived(relation, *items):
+        for item in items:
+            landing = view(relation, item)
+            pltpu.make_async_copy(landing, landing, arrive_sem.at[relation, item]).wait()
+
+    weight_copy.wait()
+    pl.semaphore_wait(barrier, 3 + (layer > 0).astype(jnp.int32) + (layer < layers - 1).astype(jnp.int32))
+    for item in (KF, VF, QF):
+        to_x(item)
+        to_y(item)
+    signal(token_sem.at[0], (partner, mp))
+
+    def tokens_step(step):
+        if step == 0:
+            pl.semaphore_wait(token_sem.at[0], 1)
+            signal(token_sem.at[1], (dp, flip(mp, 1)))
+        elif step == 1:
+            pl.semaphore_wait(token_sem.at[1], 1)
+            signal(token_sem.at[2], (dp, flip(mp, 2)))
+        else:
+            hop = step - 3
+            if hop < 0:
+                pl.semaphore_wait(token_sem.at[2], 1)
+            else:
+
+                @pl.when(layer == hop + 1)
+                def _():
+                    pl.semaphore_wait(token_sem.at[3], 1)
+
+                @pl.when(layer == layers - 2 - hop)
+                def _():
+                    pl.semaphore_wait(token_sem.at[4], 1)
+
+            if hop + 1 < layers - 1:
+
+                @pl.when(layer == hop + 1)
+                def _():
+                    signal(token_sem.at[3], (dp + 2, mp))
+
+                @pl.when(layer == layers - 2 - hop)
+                def _():
+                    signal(token_sem.at[4], (dp - 2, mp))
+
+    eye = lax.broadcasted_iota(jnp.int32, (masks, masks), 0) == lax.broadcasted_iota(
+        jnp.int32, (masks, masks), 1
+    )
+    places = lax.broadcasted_iota(jnp.int32, (masks, seq_span), 1).astype(f32)
+
+    def locate(which):
+        length = lengths_ref[sequence_ref[which]].astype(f32)
+        codes = codes_ref[pl.ds(which, 1), :].astype(f32)
+        quotient = jnp.floor(codes / length)
+        spots = codes - quotient * length
+        spots = jnp.where(spots < 0.0, spots + length, spots)
+        spots = jnp.where(spots >= length, spots - length, spots)
+        spots = jnp.sum(jnp.where(eye, spots, 0.0), axis=1, keepdims=True)
+        live = lax.broadcasted_iota(jnp.int32, (1, seq_span), 1).astype(f32) < length
+        return places == spots, live
+
+    chosen, own_alive = locate(me)
+    mate_chosen, mate_alive = locate(mate)
+    alive = (own_alive, mate_alive)
+    tokens = tokens_ref[pl.ds(sequence_ref[me], 1), :].astype(f32)
+    targets = jnp.sum(jnp.where(chosen, tokens, 0.0), axis=1, keepdims=True)
+    onehot = jnp.where(chosen, 1.0, 0.0).astype(bf16)
+    both = jnp.concatenate([onehot, jnp.where(mate_chosen, 1.0, 0.0).astype(bf16)], axis=0)
+
+    hidden_copy.wait()
+    tile = 128
+
+    def norm_copy(step):
+        rows = pl.ds(pl.multiple_of(step * tile, tile), tile)
+        return pltpu.make_async_remote_copy(
+            src_ref=normed.at[0, rows, :],
+            dst_ref=normed.at[1, rows, :],
+            send_sem=norm_send_sem.at[step],
+            recv_sem=norm_sem.at[step],
+            device_id=(partner, mp),
+            device_id_type=MESH,
+        )
+
+    def norm_rows(step, carry):
+        rows = pl.ds(pl.multiple_of(step * tile, tile), tile)
+        normed[0, rows, :] = (layer_norm(hidden[rows, :].astype(f32)) * gain_ref[...].reshape(1, feature)).astype(bf16)
+        return carry
+
+    lax.fori_loop(0, seq_span // tile, norm_rows, 0)
+    for step in range(seq_span // tile):
+        norm_copy(step).start()
+    rows_buf[0] = jnp.dot(onehot, normed[0], preferred_element_type=f32).astype(bf16)
+    mixed[:masks, :] = jnp.dot(onehot, hidden[...], preferred_element_type=f32)
+    mixed[masks:, :] = jnp.zeros((masks, feature), f32)
+    rows_copy = pltpu.make_async_remote_copy(
+        src_ref=rows_buf.at[0],
+        dst_ref=rows_buf.at[1],
+        send_sem=swap_send_sem.at[1],
+        recv_sem=swap_sem.at[1],
+        device_id=(partner, mp),
+        device_id_type=MESH,
+    )
+    rows_copy.start()
+    split_copy.wait()
+    table = jnp.dot(both, split[...], preferred_element_type=f32)
+    query_cos = table[:, :LANES] + table[:, LANES : 2 * LANES]
+    query_sin = table[:, 2 * LANES : 3 * LANES] + table[:, 3 * LANES :]
+    lane = lax.broadcasted_iota(jnp.int32, (1, LANES), 1)
+    first = lane % head_size < head_size // 2
+    low = lane < head_size
+    transposed = (((1,), (1,)), ((), ()))
+
+    def rotate(inputs, cosine, sine):
+        turned = jnp.where(
+            first,
+            pltpu.roll(inputs, LANES - head_size // 2, 1),
+            pltpu.roll(inputs, head_size // 2, 1),
+        )
+        return inputs * cosine + turned * sine
+
+    span = seq_span // 2
+
+    def stack(refs):
+        return jnp.concatenate([ref[...] for ref in refs], axis=0)
+
+    def weights_of(unit):
+        keys = []
+        for relation, item in unit:
+            start = head_of(item) * head_rows + head_size
+            keys.append(wbuf.at[relation, pl.ds(pl.multiple_of(start, head_size), 2 * head_size), :])
+        return keys
+
+    def project(unit, buffer, low_slot, high_slot):
+        keys = stack(weights_of(unit))
+
+        def step_of(step, carry):
+            slot = step // 2
+            rows = pl.ds(pl.multiple_of((step % 2) * span, 16), span)
+            made = lax.dot_general(normed[slot, rows, :], keys, transposed, preferred_element_type=f32)
+            for head in range(2):
+                block = made[:, head * LANES : (head + 1) * LANES]
+                block = jnp.where(low, rotate(block, cos[rows, :], sin[rows, :]), block)
+                pbuf[buffer, slot, rows, head * LANES : (head + 1) * LANES] = block.astype(bf16)
+            return carry
+
+        lax.fori_loop(2 * low_slot, 2 * high_slot, step_of, 0)
+
+    def queries(unit, low_slot, high_slot):
+        weights = stack([view(relation, item - item % 4 + QF) for relation, item in unit])
+        rows = slice(low_slot * masks, high_slot * masks)
+        source = rows_buf[low_slot:high_slot].reshape((high_slot - low_slot) * masks, feature)
+        made = lax.dot_general(source, weights, transposed, preferred_element_type=f32)
+        return rotate(made * head_size ** (-0.5), query_cos[rows], query_sin[rows])
+
+    def attend(which, buffer, slot, query):
+        empty = jnp.zeros((masks, LANES), bf16)
+        near = jnp.where(low, query, 0.0).astype(bf16)
+        far = jnp.where(low, pltpu.roll(query, head_size, 1), 0.0).astype(bf16)
+        pair = jnp.concatenate(
+            [jnp.concatenate([near, empty], axis=1), jnp.concatenate([empty, far], axis=1)], axis=0
+        )
+        block = pbuf[buffer, slot]
+        logits = lax.dot_general(pair, block, transposed, preferred_element_type=f32)
+        logits = jnp.where(alive[slot], logits, -1e30)
+        weight = jnp.exp(logits - jnp.max(logits, axis=-1, keepdims=True))
+        probs = (weight / jnp.sum(weight, axis=-1, keepdims=True)).astype(bf16)
+        vectors = jnp.dot(probs, block, preferred_element_type=f32)
+        total = jnp.where(low, pltpu.roll(vectors[:masks, :LANES], head_size, 1), vectors[masks:, LANES:])
+        context[slot * masks : (slot + 1) * masks, which * LANES : (which + 1) * LANES] = total.astype(bf16)
+
+    def attend_both(which, unit, buffer):
+        query = queries(unit, 0, 2)
+        for slot in range(2):
+            attend(which, buffer, slot, query[slot * masks : (slot + 1) * masks])
+
+    def mix(units):
+        out_weights = stack([view(relation, item - item % 4 + OF) for unit in units.values() for relation, item in unit])
+        lo, hi = min(units), max(units) + 1
+        mixed[...] += jnp.dot(context[:, lo * LANES : hi * LANES], out_weights, preferred_element_type=f32)
+
+    own = ((0, KF), (0, KS))
+    firsts = ((1, KF), (2, KF))
+    seconds = ((1, KS), (2, KS))
+    across = ((3, KF), (3, KS))
+
+    cos_copy.wait()
+    sin_copy.wait()
+    project(own, 0, 0, 1)
+    attend(0, 0, 0, queries(own, 0, 1))
+    arrived(1, KF)
+    to_z(KF, 1)
+    arrived(2, KF)
+    to_z(KF, 2)
+    to_x(KF, 2)
+    tokens_step(0)
+    for step in range(seq_span // tile):
+        norm_copy(step).wait_recv()
+    rows_copy.wait_recv()
+    project(own, 0, 1, 2)
+    arrived(1, VF)
+    to_z(VF, 1)
+    arrived(2, VF)
+    to_z(VF, 2)
+    to_x(VF, 2)
+    to_x(QS)
+    out_weight_copy.wait()
+    to_x(OF)
+    attend(0, 0, 1, queries(own, 1, 2))
+    tokens_step(1)
+    mix({0: own})
+    project(firsts, 1, 0, 2)
+    arrived(1, QF)
+    to_y(QF, 1)
+    to_y(QS)
+    arrived(2, QF)
+    tokens_step(2)
+    attend_both(1, firsts, 1)
+    arrived(1, KS)
+    to_y(KS, 1)
+    arrived(3, KF)
+    arrived(2, KS)
+    tokens_step(3)
+    arrived(1, VS)
+    arrived(2, VS)
+    project(seconds, 0, 0, 2)
+    arrived(3, VF)
+    to_z(VF, 3)
+    arrived(1, QS)
+    to_y(QS, 1)
+    to_y(OF)
+    arrived(2, QS)
+    tokens_step(4)
+    attend_both(2, seconds, 0)
+    arrived(1, OF)
+    to_z(OF, 1)
+    arrived(3, QF)
+    arrived(3, VS)
+    tokens_step(5)
+    arrived(3, KS)
+    project(across, 1, 0, 2)
+    arrived(2, OF)
+    to_z(OF, 2)
+    to_x(OF, 2)
+    arrived(3, QS)
+    attend_both(3, across, 1)
+    arrived(3, OF)
+    to_z(OF, 3)
+    for relation in (1, 2, 3):
+        arrived(relation, OS)
+    mix({1: firsts, 2: seconds, 3: across})
+    inbox_copy = pltpu.make_async_remote_copy(
+        src_ref=mixed.at[pl.ds(masks, masks), :],
+        dst_ref=inbox,
+        send_sem=swap_send_sem.at[0],
+        recv_sem=swap_sem.at[0],
+        device_id=(partner, mp),
+        device_id_type=MESH,
+    )
+    inbox_copy.start()
+    dense_copy.wait()
+    for step in range(seq_span // tile):
+        norm_copy(step).wait_send()
+    rows_copy.wait_send()
+    for copy in sent:
+        copy.wait_send()
+    inbox_copy.wait_recv()
+    residual = mixed[:masks, :] + inbox[...]
+    normed_final = (layer_norm(residual) * final_gain_ref[...].reshape(1, feature)).astype(bf16)
+    dense_out = jnp.dot(normed_final, dense[...], preferred_element_type=f32)
+    headed = layer_norm(0.5 * dense_out * (1.0 + lax.erf(dense_out * 0.5**0.5))).astype(bf16)
+    logits = lax.dot_general(headed, decoder_ref[...], transposed, preferred_element_type=f32) + bias_ref[...]
+    largest = jnp.max(logits, axis=-1, keepdims=True)
+    scale = jnp.log(jnp.sum(jnp.exp(logits - largest), axis=-1, keepdims=True)) + largest
+    vocabulary = lax.broadcasted_iota(jnp.int32, logits.shape, 1).astype(f32)
+    picked = jnp.sum(jnp.where(vocabulary == targets, logits - scale, 0.0), axis=1, keepdims=True)
+    row = jnp.sum(jnp.where(eye, picked, 0.0), axis=0, keepdims=True)
+    padded = jnp.pad(row, ((0, 0), (0, LANES - masks)))
+    scores[me] = jnp.broadcast_to(padded, scores.shape[1:])
+
+    def score_copy(step):
+        other = (me + step) % devices
+        return pltpu.make_async_remote_copy(
+            src_ref=scores.at[me, pl.ds(0, 1), :],
+            dst_ref=scores.at[me, pl.ds(0, 1), :],
+            send_sem=score_send_sem.at[step],
+            recv_sem=score_sem.at[me],
+            device_id=(other // n_mp, other % n_mp),
+            device_id_type=MESH,
+        )
+
+    def send_scores(step, carry):
+        score_copy(step).start()
+        return carry
+
+    lax.fori_loop(1, devices, send_scores, 0)
+    inbox_copy.wait_send()
+
+    def wait_scores(step, carry):
+        source = (me + step) % devices
+        landing = scores.at[source, pl.ds(0, 1), :]
+        pltpu.make_async_copy(landing, landing, score_sem.at[source]).wait()
+        return carry
+
+    lax.fori_loop(1, devices, wait_scores, 0)
+
+    def wait_sends(step, carry):
+        score_copy(step).wait_send()
+        return carry
+
+    lax.fori_loop(1, devices, wait_sends, 0)
+    group = out_ref.shape[0]
+    wanted = dp * group + lax.broadcasted_iota(jnp.int32, (group, owner_ref.shape[1]), 0)
+    select = jnp.where(owner_ref[...] == wanted, 1.0, 0.0)
+    out_ref[...] = jnp.dot(select, scores[:, 0, :], preferred_element_type=f32, precision=lax.Precision.HIGHEST)
+
+
+def split_call(shape, inputs, weight, out_weight, hidden, dense_weight, cosine, sine, group, head_size):
+    n_dp, n_mp = shape
+    devices = n_dp * n_mp
+    seq_span, feature = hidden.shape
+    width = weight.shape[1]
+    masks = inputs[2].shape[1]
+    high = [t.astype(jnp.bfloat16).astype(np.float32) for t in (cosine, sine)]
+    parts = [high[0], cosine - high[0], high[1], sine - high[1]]
+    split = np.concatenate(parts, axis=1).astype(jnp.bfloat16)
+    dma = pltpu.SemaphoreType.DMA
+    vmem = pl.BlockSpec(memory_space=pltpu.VMEM)
+    smem = pl.BlockSpec(memory_space=pltpu.SMEM)
+    anywhere = pl.BlockSpec(memory_space=pl.ANY)
+    tiles = seq_span // 128
+    return pl.pallas_call(
+        functools.partial(split_kernel, (n_dp, n_mp, head_size)),
+        name="score_split",
+        out_shape=jax.ShapeDtypeStruct((group, LANES), f32),
+        in_specs=[smem] * 2 + [vmem] * 7 + [anywhere] * 7,
+        out_specs=vmem,
+        scratch_shapes=[
+            pltpu.VMEM((seq_span, feature), bf16),
+            pltpu.VMEM((2, seq_span, feature), bf16),
+            pltpu.VMEM((2, masks, feature), bf16),
+            pltpu.VMEM((n_mp, width, feature), bf16),
+            pltpu.VMEM((n_mp, 2 * head_size, feature), bf16),
+            pltpu.VMEM((feature, feature), bf16),
+            pltpu.VMEM((seq_span, LANES), f32),
+            pltpu.VMEM((seq_span, LANES), f32),
+            pltpu.VMEM((seq_span, 4 * LANES), bf16),
+            pltpu.VMEM((2, 2, seq_span, 2 * LANES), bf16),
+            pltpu.VMEM((2 * masks, 4 * LANES), bf16),
+            pltpu.VMEM((2 * masks, feature), f32),
+            pltpu.VMEM((masks, feature), f32),
+            pltpu.VMEM((devices, 8, LANES), f32),
+            dma((7,)),
+            dma((32,)),
+            dma((n_mp, 8)),
+            dma((tiles,)),
+            dma((tiles,)),
+            dma((2,)),
+            dma((2,)),
+            dma((devices,)),
+            dma((devices,)),
+            pltpu.SemaphoreType.REGULAR((5,)),
+        ],
+        compiler_params=pltpu.CompilerParams(collective_id=1, has_side_effects=True),
+    )(
+        *inputs,
+        hidden,
+        weight,
+        out_weight,
+        dense_weight,
+        jnp.asarray(cosine),
+        jnp.asarray(sine),
+        jnp.asarray(split),
+    )
+
+
 def on_device(
     shape,
     hidden_states,
@@ -471,6 +970,22 @@
     vmem = pl.BlockSpec(memory_space=pltpu.VMEM)
     smem = pl.BlockSpec(memory_space=pltpu.SMEM)
     anywhere = pl.BlockSpec(memory_space=pl.ANY)
+    own = masks // n_mp
+    inputs = (
+        copy_sequence,
+        seq_lengths,
+        mask_code,
+        seq_tokens,
+        copy_owner.reshape(1, -1),
+        ln_attn_gain,
+        ln_final_gain,
+        decoder_weight.T,
+        decoder_bias.reshape(1, -1),
+    )
+    if n_mp == 4 and n_dp == 8 and heads == 4 and seq_span % 128 == 0:
+        hidden = hidden_states.reshape(seq_span, feature)
+        rows = split_call(shape, inputs, weight, out_weight, hidden, dense_weight, cosine, sine, group, head_size)
+        return lax.dynamic_slice_in_dim(rows, lax.axis_index("mp") * own, own, 1)
     rows = pl.pallas_call(
         functools.partial(kernel, (n_dp, n_mp, head_size, in_chunk, chunks)),
         name="score_copies",
@@ -517,7 +1032,6 @@
         jnp.asarray(cosine),
         jnp.asarray(sine),
     )
-    own = masks // n_mp
     return lax.dynamic_slice_in_dim(rows, lax.axis_index("mp") * own, own, 1)
 
 

time: 57 us -> 58.9 us (1.033)
  Pallas kernels: 53.5 us -> 55.4 us
    pallas_call x1, Pallas kernels: 53.5 us -> 55.4 us  [split_call(): pl.pallas_call(functools.partial(split_kernel, (n_dp, n_mp, head_size)),...]
where the time goes in v1:
time: 58.9 us; the launch traced here: 58.7 us
  Pallas kernels  55.4 us (94%)
  local copies, waits for them, and re-layouts  3.27 us (6%)
    pallas_call x1, Pallas kernels, split_call(): pl.pallas_call(functools.partial(split_kernel, (n_dp, n_mp, head_size)),...  55.4 us
    transpose x1, local copies, waits for them, and re-layouts, on_device(): jnp.swapaxes(output_weight, 0, 1).reshape(heads * head_size, feature)  1.99 us
    dynamic_slice x1, local copies, waits for them, and re-layouts, on_device(): return lax.dynamic_slice_in_dim(rows, lax.axis_index('mp') * own, own, 1)  1.29 us

profile of v1, /device:TPU:0, one launch (start us, length us, event | category | flops | bytes accessed | tf_op | source)
XLA Modules:
  0.0 58.7 jit_solution(1769744805122751572)
XLA Ops:
  0.0 2.0 %copy.17 = bf16[4,64,1280]{2,1,0:T(8,128)(2,1)} copy(bf16[4,64,1280]{2,0,1:T(4,128)(2,1)} %bitcast.12) | data formatting | bytes 1310720 | tf_op jit(solution)/shard_map/transpose | solution.py:965
  2.0 55.4 %score_split.1 = f32[4,128]{1,0:T(4,128)} custom-call(s32[32]{0:T(128)} %sequence_ref.1, s32[24]{0:T(128)} %lengths_ref.1, s32[32,64]{1,0:T(8,128)} %codes_ref.1, s32[24,640]{1,0:T(8,128)} %tokens_ref.1, s32[1,32]{1,0:T(1,128)} %bitcast.14, f32[1280]{0:T(1024)} %gain_ref.1, f32[1280]{0:T(1024)} %final_gain_ref.1, bf16[33,1280]{1,0:T(8,128)(2,1)} %bitcast.13, ...), custom_call_target="tpu_custom_call" | custom-call | tf_op jit(solution)/shard_map/score_split/pallas_call | solution.py:893
  57.4 1.3 %constant_dynamic-slice_fusion = f32[4,16]{1,0:T(4,128)} fusion(f32[4,128]{1,0:T(4,128)} %score_split.1, s32[]{:T(128)S(6)} %select_n.3), kind=kLoop, calls=%fused_computation | loop fusion | bytes 516 | tf_op jit(solution)/shard_map/dynamic_slice | solution.py:988

commit v2 on v1

--- a/solution.py
+++ b/solution.py
@@ -436,7 +436,73 @@
     out_ref[...] = jnp.dot(select, scores[:, 0, :], **exact)
 
 
-KF, VF, QF, OF, KS, VS, QS, OS = range(8)
+ITEMS = {"K0": 0, "V0": 1, "K1": 2, "V1": 3, "Q0": 4, "Q1": 5, "O0": 6, "O1": 7}
+FIRST_ROW = {"Q": 0, "K": 64, "V": 128}
+ENDS = [('0V0.1>xy', '0V0.0>xy', '0K0.1>xy', '0O0.0>y', '0O0.1>x'),
+ ('0K0.0>xy',
+  '0R',
+  '2V0.1>e',
+  '1K0.1>e',
+  '2O0.0>x',
+  '0O0.1>y',
+  '1V0.1>ey',
+  '2K0.0>ex',
+  '3V0.1',
+  '0O1.0>xy',
+  '1V0.0>ey'),
+ ('1K0.0>e', '0O0.0>x'),
+ ('1K1.1>y', '1O0.1', '1O1.0', '2K0.1>ex', '1K1.0>y'),
+ ('1V1.0', '2O0.1>x'),
+ ('2V1.0', '2V0.0>e'),
+ ('2K1.0', '3K0.0>e', '3K0.1>e'),
+ ('2G', '0O1.1>xy', '2V1.1', '1G', '3V0.0'),
+ ('3O0.1>e', '3K1.1', '2K1.1', '1V1.1'),
+ (),
+ ('2O1.0', '3V1.1', '3K1.0'),
+ ('3V1.0', '3O0.0>e'),
+ ('2O1.1', '1O0.0'),
+ ('3G', '1O1.1', '3O1.1'),
+ ('3O1.0',)]
+MIDS = [('0ox.1>y', '0V1.0>x', '0qx.1>y', '0K1.1>x', '0K1.0>x'),
+ ('0V1.0>y',
+  '0K1.0>y',
+  '0qx.1>x',
+  '0qx.0>x',
+  '1V1.0>e',
+  '2ox.1>m',
+  '1K1.1>e',
+  '0V1.1>y',
+  '0qx.0>y',
+  '2qx.1>m',
+  '2V1.0>ex',
+  '0V1.1>x',
+  '0ox.0>x',
+  '0ox.0>y'),
+ ('9R', '1K1.0>e', '1qx.1>my', '1qx.0>my', '2oy.1', '2O1!1>x', '2K1.0>e', '2V1.1>ex'),
+ (),
+ ('2qx.0>m', '2ox.0>m', '1V1.1>e', '3V1.0>e', '2K0.0', '1V0.1', '0ox.1>x', '2qy.1', '0K1.1>y'),
+ ('3qx.1>m',
+  '1qy.1',
+  '2V0.1',
+  '1qy.0',
+  'q1',
+  '2qy.0',
+  '1V0.0',
+  '3qx.0>m',
+  '1kx!1>y',
+  'q2',
+  '1kx!0>y',
+  '2K1.1>e',
+  '1ox.0>m'),
+ ('3V1.1>e',),
+ ('1K0.1', '3kx.1>m', '2oy.0', '2O1!0>x', '3O1.1>e', '3qy.0', '3qy.1'),
+ ('q3', '3kx.0>m', '2V0.0', '1ox.1>m', '2K0.1', '1K0.0'),
+ (),
+ ('3O1.0>e', '3K0.0', '3ky.1'),
+ ('3K0.1', '3ky.0', '1oy.0'),
+ (),
+ (),
+ ('1oy.1', '3O0.0', '3O0.1')]
 
 
 def split_kernel(
@@ -469,12 +535,15 @@
     split,
     pbuf,
     context,
+    qbuf,
+    gbuf,
     mixed,
     inbox,
     scores,
     local_sem,
     send_sem,
     arrive_sem,
+    query_sem,
     norm_send_sem,
     norm_sem,
     swap_send_sem,
@@ -494,27 +563,27 @@
     me = dp * n_mp + mp
     mate = partner * n_mp + mp
     parity = layer % 2
-    above = dp + 2 - 4 * parity
+    pair = dp + 2 - 4 * parity
+    twin = dp - 2 + 4 * parity
+    middle = jnp.logical_and(layer > 0, layer < layers - 1)
+    side = 1 - parity
     seq_span, feature = hidden.shape
     masks = codes_ref.shape[1]
     head_rows = 3 * head_size
+    half_rows = head_size // 2
+    where = {"x": (dp, flip(mp, 1)), "y": (dp, flip(mp, 2)), "e": (pair, mp), "m": (twin, mp), "d": (partner, mp)}
 
     barrier = pltpu.get_barrier_semaphore()
 
-    def signal(semaphore, where):
-        pl.semaphore_signal(semaphore, inc=1, device_id=where, device_id_type=MESH)
-
-    signal(barrier, (partner, mp))
-    signal(barrier, (dp, flip(mp, 1)))
-    signal(barrier, (dp, flip(mp, 2)))
-
-    @pl.when(layer > 0)
+    def signal(semaphore, target):
+        pl.semaphore_signal(semaphore, inc=1, device_id=target, device_id_type=MESH)
+
+    for link in "dxye":
+        signal(barrier, where[link])
+
+    @pl.when(middle)
     def _():
-        signal(barrier, (dp - 2, mp))
-
-    @pl.when(layer < layers - 1)
-    def _():
-        signal(barrier, (dp + 2, mp))
+        signal(barrier, where["m"])
 
     def local(index, source, target):
         copy = pltpu.make_async_copy(source, target, local_sem.at[index])
@@ -522,56 +591,112 @@
         return copy
 
     weight_copy = local(1, weight_hbm.at[core], wbuf.at[0])
+    out_start = pl.multiple_of(core * 2 * head_size, 2 * head_size)
+    out_weight_copy = local(2, out_weight_hbm.at[pl.ds(out_start, 2 * head_size), :], obuf.at[0])
     hidden_copy = local(0, hidden_hbm, hidden)
     cos_copy = local(3, cos_hbm, cos)
     sin_copy = local(4, sin_hbm, sin)
     split_copy = local(6, split_hbm, split)
-    out_weight_copy = local(2, out_weight_hbm.at[pl.ds(pl.multiple_of(core * 2 * head_size, 128), 2 * head_size), :], obuf.at[0])
     dense_copy = local(5, dense_hbm, dense)
 
-    def head_of(item):
-        return parity if item < KS else 1 - parity
-
-    def view(relation, item):
-        head, kind = head_of(item), item % 4
-        if kind == OF:
-            return obuf.at[relation, pl.ds(pl.multiple_of(head * head_size, head_size), head_size), :]
-        start = head * head_rows + (head_size, 2 * head_size, 0)[kind]
-        return wbuf.at[relation, pl.ds(pl.multiple_of(start, head_size), head_size), :]
-
-    sent = []
-
-    def send(source_relation, item, relation, landing, where):
-        copy = pltpu.make_async_remote_copy(
-            src_ref=view(source_relation, item),
-            dst_ref=view(source_relation ^ relation if relation != 4 else source_relation, item),
-            send_sem=send_sem.at[len(sent)],
-            recv_sem=arrive_sem.at[source_relation ^ relation if relation != 4 else source_relation, landing],
-            device_id=where,
+    def number(item):
+        if item in ITEMS:
+            return ITEMS[item]
+        return {"qx": 4 + side, "qy": 5 - side, "ox": 6 + side, "oy": 7 - side, "kx": 2 - side, "ky": 1 + side}[item]
+
+    def view(relation, item, half):
+        if item in ITEMS:
+            kind, head = item[0], int(item[1])
+            start = head * head_size if kind == "O" else head * head_rows + FIRST_ROW[kind]
+        elif item[0] == "k":
+            kind = "K"
+            start = 256 - 128 * side if item == "kx" else 128 + 128 * side
+        else:
+            kind = item[0].upper()
+            start = (side if item[1] == "x" else 1 - side) * (head_rows if kind == "Q" else head_size)
+        rows = pl.ds(pl.multiple_of(start + half * half_rows, half_rows), half_rows)
+        return (obuf if kind == "O" else wbuf).at[relation, rows, :]
+
+    flips = {"x": 1, "y": 2, "e": 0, "m": 0}
+
+    def piece_copy(relation, item, half, link, index):
+        target = relation ^ flips[link]
+        return pltpu.make_async_remote_copy(
+            src_ref=view(relation, item, half),
+            dst_ref=view(target, item, half),
+            send_sem=send_sem.at[index],
+            recv_sem=arrive_sem.at[target, 2 * number(item) + half],
+            device_id=where[link],
             device_id_type=MESH,
         )
-        copy.start()
-        sent.append(copy)
-
-    def to_x(item, source_relation=0):
-        send(source_relation, item, 1, item, (dp, flip(mp, 1)))
-
-    def to_y(item, source_relation=0):
-        send(source_relation, item, 2, item, (dp, flip(mp, 2)))
-
-    def to_z(item, source_relation):
-        send(source_relation, item, 4, item + 4, (above, mp))
-
-    def arrived(relation, *items):
-        for item in items:
-            landing = view(relation, item)
-            pltpu.make_async_copy(landing, landing, arrive_sem.at[relation, item]).wait()
+
+    def rows_copy(source, target, link, index):
+        return pltpu.make_async_remote_copy(
+            src_ref=rows_buf.at[source],
+            dst_ref=rows_buf.at[target],
+            send_sem=swap_send_sem.at[index],
+            recv_sem=swap_sem.at[index],
+            device_id=where[link],
+            device_id_type=MESH,
+        )
+
+    def query_copy(relation):
+        return pltpu.make_async_remote_copy(
+            src_ref=gbuf.at[relation],
+            dst_ref=qbuf.at[relation],
+            send_sem=query_sem.at[0, relation],
+            recv_sem=query_sem.at[1, relation],
+            device_id=where["e"],
+            device_id_type=MESH,
+        )
+
+    sent = {True: [], False: []}
+
+    def serve(words, in_middle):
+        for word in words:
+            if word in ("q1", "q2", "q3"):
+                project_queries(int(word[1]))
+                continue
+            name, _, links = word.partition(">")
+            relation, item = int(name[0]), name[1:3]
+            if item == "R":
+                if in_middle:
+                    rows_copy(0, 2, "e", 1).wait_recv()
+                    rows_copy(2, 3, "d", 2).start()
+                else:
+                    rows_copy(0, 2, "e", 1).start()
+                continue
+            if item == "G":
+                query_copy(relation).wait_recv()
+                continue
+            half = int(name[4])
+            if relation and name[3] != "!":
+                landing = view(relation, item, half)
+                pltpu.make_async_copy(
+                    landing, landing, arrive_sem.at[relation, 2 * number(item) + half]
+                ).wait()
+            for link in links:
+                index = len(sent[in_middle])
+                sent[in_middle].append((relation, item, half, link, index))
+                piece_copy(relation, item, half, link, index).start()
+
+    def service(index):
+        if MIDS[index]:
+
+            @pl.when(middle)
+            def _():
+                serve(MIDS[index], True)
+
+        if ENDS[index]:
+
+            @pl.when(jnp.logical_not(middle))
+            def _():
+                serve(ENDS[index], False)
 
     weight_copy.wait()
-    pl.semaphore_wait(barrier, 3 + (layer > 0).astype(jnp.int32) + (layer < layers - 1).astype(jnp.int32))
-    for item in (KF, VF, QF):
-        to_x(item)
-        to_y(item)
+    out_weight_copy.wait()
+    pl.semaphore_wait(barrier, 4 + middle.astype(jnp.int32))
+    service(0)
     signal(token_sem.at[0], (partner, mp))
 
     def tokens_step(step):
@@ -621,13 +746,13 @@
         live = lax.broadcasted_iota(jnp.int32, (1, seq_span), 1).astype(f32) < length
         return places == spots, live
 
-    chosen, own_alive = locate(me)
-    mate_chosen, mate_alive = locate(mate)
-    alive = (own_alive, mate_alive)
+    located = [locate(which) for which in (me, mate, pair * n_mp + mp, (pair + 1 - 2 * core) * n_mp + mp)]
+    chosen = located[0][0]
+    alive = [live for _, live in located]
     tokens = tokens_ref[pl.ds(sequence_ref[me], 1), :].astype(f32)
     targets = jnp.sum(jnp.where(chosen, tokens, 0.0), axis=1, keepdims=True)
-    onehot = jnp.where(chosen, 1.0, 0.0).astype(bf16)
-    both = jnp.concatenate([onehot, jnp.where(mate_chosen, 1.0, 0.0).astype(bf16)], axis=0)
+    onehots = [jnp.where(spots, 1.0, 0.0).astype(bf16) for spots, _ in located]
+    onehot = onehots[0]
 
     hidden_copy.wait()
     tile = 128
@@ -649,22 +774,14 @@
         return carry
 
     lax.fori_loop(0, seq_span // tile, norm_rows, 0)
+    rows_buf[0] = jnp.dot(onehot, normed[0], preferred_element_type=f32).astype(bf16)
     for step in range(seq_span // tile):
         norm_copy(step).start()
-    rows_buf[0] = jnp.dot(onehot, normed[0], preferred_element_type=f32).astype(bf16)
     mixed[:masks, :] = jnp.dot(onehot, hidden[...], preferred_element_type=f32)
     mixed[masks:, :] = jnp.zeros((masks, feature), f32)
-    rows_copy = pltpu.make_async_remote_copy(
-        src_ref=rows_buf.at[0],
-        dst_ref=rows_buf.at[1],
-        send_sem=swap_send_sem.at[1],
-        recv_sem=swap_sem.at[1],
-        device_id=(partner, mp),
-        device_id_type=MESH,
-    )
-    rows_copy.start()
+    rows_copy(0, 1, "d", 0).start()
     split_copy.wait()
-    table = jnp.dot(both, split[...], preferred_element_type=f32)
+    table = jnp.dot(jnp.concatenate(onehots, axis=0), split[...], preferred_element_type=f32)
     query_cos = table[:, :LANES] + table[:, LANES : 2 * LANES]
     query_sin = table[:, 2 * LANES : 3 * LANES] + table[:, 3 * LANES :]
     lane = lax.broadcasted_iota(jnp.int32, (1, LANES), 1)
@@ -685,19 +802,16 @@
     def stack(refs):
         return jnp.concatenate([ref[...] for ref in refs], axis=0)
 
-    def weights_of(unit):
-        keys = []
-        for relation, item in unit:
-            start = head_of(item) * head_rows + head_size
-            keys.append(wbuf.at[relation, pl.ds(pl.multiple_of(start, head_size), 2 * head_size), :])
-        return keys
-
-    def project(unit, buffer, low_slot, high_slot):
-        keys = stack(weights_of(unit))
+    def rows_of(start, count):
+        return pl.ds(start if isinstance(start, int) else pl.multiple_of(start, head_size), count)
+
+    def project(unit, buffer, slot):
+        keys = stack(
+            [wbuf.at[relation, rows_of(head * head_rows + head_size, 2 * head_size), :] for relation, head in unit]
+        )
 
         def step_of(step, carry):
-            slot = step // 2
-            rows = pl.ds(pl.multiple_of((step % 2) * span, 16), span)
+            rows = pl.ds(pl.multiple_of(step * span, 16), span)
             made = lax.dot_general(normed[slot, rows, :], keys, transposed, preferred_element_type=f32)
             for head in range(2):
                 block = made[:, head * LANES : (head + 1) * LANES]
@@ -705,24 +819,38 @@
                 pbuf[buffer, slot, rows, head * LANES : (head + 1) * LANES] = block.astype(bf16)
             return carry
 
-        lax.fori_loop(2 * low_slot, 2 * high_slot, step_of, 0)
-
-    def queries(unit, low_slot, high_slot):
-        weights = stack([view(relation, item - item % 4 + QF) for relation, item in unit])
+        lax.fori_loop(0, seq_span // span, step_of, 0)
+
+    def queries(relation, low_slot, high_slot):
+        weights = stack([wbuf.at[relation, head * head_rows : head * head_rows + head_size, :] for head in range(2)])
         rows = slice(low_slot * masks, high_slot * masks)
         source = rows_buf[low_slot:high_slot].reshape((high_slot - low_slot) * masks, feature)
         made = lax.dot_general(source, weights, transposed, preferred_element_type=f32)
-        return rotate(made * head_size ** (-0.5), query_cos[rows], query_sin[rows])
-
-    def attend(which, buffer, slot, query):
+        return rotate(made * head_size ** (-0.5), query_cos[rows], query_sin[rows]).astype(bf16)
+
+    def project_queries(relation):
+        if relation == 1:
+            rows_copy(2, 3, "d", 2).wait_recv()
+        made = queries(relation, 0, 4)
+        gbuf[relation] = made[2 * masks :]
+        qbuf[relation] = made[: 2 * masks]
+        query_copy(relation).start()
+
+    def of_head(query, head):
+        query = query.astype(f32)
+        if isinstance(head, int):
+            return pltpu.roll(query, head_size, 1) if head else query
+        return jnp.where(head == 1, pltpu.roll(query, head_size, 1), query)
+
+    def attend(which, buffer, slot, near, far):
         empty = jnp.zeros((masks, LANES), bf16)
-        near = jnp.where(low, query, 0.0).astype(bf16)
-        far = jnp.where(low, pltpu.roll(query, head_size, 1), 0.0).astype(bf16)
-        pair = jnp.concatenate(
+        near = jnp.where(low, near, 0.0).astype(bf16)
+        far = jnp.where(low, far, 0.0).astype(bf16)
+        both = jnp.concatenate(
             [jnp.concatenate([near, empty], axis=1), jnp.concatenate([empty, far], axis=1)], axis=0
         )
         block = pbuf[buffer, slot]
-        logits = lax.dot_general(pair, block, transposed, preferred_element_type=f32)
+        logits = lax.dot_general(both, block, transposed, preferred_element_type=f32)
         logits = jnp.where(alive[slot], logits, -1e30)
         weight = jnp.exp(logits - jnp.max(logits, axis=-1, keepdims=True))
         probs = (weight / jnp.sum(weight, axis=-1, keepdims=True)).astype(bf16)
@@ -731,90 +859,69 @@
         context[slot * masks : (slot + 1) * masks, which * LANES : (which + 1) * LANES] = total.astype(bf16)
 
     def attend_both(which, unit, buffer):
-        query = queries(unit, 0, 2)
         for slot in range(2):
-            attend(which, buffer, slot, query[slot * masks : (slot + 1) * masks])
-
-    def mix(units):
-        out_weights = stack([view(relation, item - item % 4 + OF) for unit in units.values() for relation, item in unit])
-        lo, hi = min(units), max(units) + 1
-        mixed[...] += jnp.dot(context[:, lo * LANES : hi * LANES], out_weights, preferred_element_type=f32)
-
-    own = ((0, KF), (0, KS))
-    firsts = ((1, KF), (2, KF))
-    seconds = ((1, KS), (2, KS))
-    across = ((3, KF), (3, KS))
+            rows = slice(slot * masks, (slot + 1) * masks)
+            near, far = [of_head(qbuf[relation, rows, :], head) for relation, head in unit]
+            attend(which, buffer, slot, near, far)
+
+    def mix(low_unit, *units):
+        out_weights = stack([obuf.at[relation, rows_of(head * head_size, head_size), :] for unit in units for relation, head in unit])
+        lanes = slice(low_unit * LANES, (low_unit + len(units)) * LANES)
+        mixed[...] += jnp.dot(context[:, lanes], out_weights, preferred_element_type=f32)
+
+    early = middle.astype(jnp.int32)
+    own = ((0, 0), (0, 1))
+    firsts = ((1, early), (2, early))
+    seconds = ((1, 1 - early), (2, 1 - early))
+    across = ((3, 0), (3, 1))
 
     cos_copy.wait()
     sin_copy.wait()
-    project(own, 0, 0, 1)
-    attend(0, 0, 0, queries(own, 0, 1))
-    arrived(1, KF)
-    to_z(KF, 1)
-    arrived(2, KF)
-    to_z(KF, 2)
-    to_x(KF, 2)
+    service(1)
+    project(own, 0, 0)
+    service(2)
+    query = queries(0, 0, 1)
+    attend(0, 0, 0, of_head(query, 0), of_head(query, 1))
     tokens_step(0)
+    service(3)
     for step in range(seq_span // tile):
         norm_copy(step).wait_recv()
-    rows_copy.wait_recv()
-    project(own, 0, 1, 2)
-    arrived(1, VF)
-    to_z(VF, 1)
-    arrived(2, VF)
-    to_z(VF, 2)
-    to_x(VF, 2)
-    to_x(QS)
-    out_weight_copy.wait()
-    to_x(OF)
-    attend(0, 0, 1, queries(own, 1, 2))
+    rows_copy(0, 1, "d", 0).wait_recv()
+    project(own, 0, 1)
+    service(4)
+    query = queries(0, 1, 2)
+    attend(0, 0, 1, of_head(query, 0), of_head(query, 1))
+    mix(0, own)
     tokens_step(1)
-    mix({0: own})
-    project(firsts, 1, 0, 2)
-    arrived(1, QF)
-    to_y(QF, 1)
-    to_y(QS)
-    arrived(2, QF)
+    service(5)
+    project(firsts, 1, 0)
+    service(6)
+    project(firsts, 1, 1)
     tokens_step(2)
+    service(7)
     attend_both(1, firsts, 1)
-    arrived(1, KS)
-    to_y(KS, 1)
-    arrived(3, KF)
-    arrived(2, KS)
     tokens_step(3)
-    arrived(1, VS)
-    arrived(2, VS)
-    project(seconds, 0, 0, 2)
-    arrived(3, VF)
-    to_z(VF, 3)
-    arrived(1, QS)
-    to_y(QS, 1)
-    to_y(OF)
-    arrived(2, QS)
+    service(8)
+    project(seconds, 0, 0)
+    service(9)
+    project(seconds, 0, 1)
+    service(10)
+    attend_both(2, seconds, 0)
     tokens_step(4)
-    attend_both(2, seconds, 0)
-    arrived(1, OF)
-    to_z(OF, 1)
-    arrived(3, QF)
-    arrived(3, VS)
+    service(11)
+    project(across, 1, 0)
+    service(12)
+    project(across, 1, 1)
+    service(13)
+    attend_both(3, across, 1)
     tokens_step(5)
-    arrived(3, KS)
-    project(across, 1, 0, 2)
-    arrived(2, OF)
-    to_z(OF, 2)
-    to_x(OF, 2)
-    arrived(3, QS)
-    attend_both(3, across, 1)
-    arrived(3, OF)
-    to_z(OF, 3)
-    for relation in (1, 2, 3):
-        arrived(relation, OS)
-    mix({1: firsts, 2: seconds, 3: across})
+    service(14)
+    mix(1, firsts, seconds, across)
     inbox_copy = pltpu.make_async_remote_copy(
         src_ref=mixed.at[pl.ds(masks, masks), :],
         dst_ref=inbox,
-        send_sem=swap_send_sem.at[0],
-        recv_sem=swap_sem.at[0],
+        send_sem=swap_send_sem.at[3],
+        recv_sem=swap_sem.at[3],
         device_id=(partner, mp),
         device_id_type=MESH,
     )
@@ -822,9 +929,22 @@
     dense_copy.wait()
     for step in range(seq_span // tile):
         norm_copy(step).wait_send()
-    rows_copy.wait_send()
-    for copy in sent:
-        copy.wait_send()
+    rows_copy(0, 1, "d", 0).wait_send()
+
+    @pl.when(middle)
+    def _():
+        for record in sent[True]:
+            piece_copy(*record).wait_send()
+        rows_copy(2, 3, "d", 2).wait_send()
+        for relation in (1, 2, 3):
+            query_copy(relation).wait_send()
+
+    @pl.when(jnp.logical_not(middle))
+    def _():
+        for record in sent[False]:
+            piece_copy(*record).wait_send()
+        rows_copy(0, 2, "e", 1).wait_send()
+
     inbox_copy.wait_recv()
     residual = mixed[:masks, :] + inbox[...]
     normed_final = (layer_norm(residual) * final_gain_ref[...].reshape(1, feature)).astype(bf16)
@@ -899,7 +1019,7 @@
         scratch_shapes=[
             pltpu.VMEM((seq_span, feature), bf16),
             pltpu.VMEM((2, seq_span, feature), bf16),
-            pltpu.VMEM((2, masks, feature), bf16),
+            pltpu.VMEM((4, masks, feature), bf16),
             pltpu.VMEM((n_mp, width, feature), bf16),
             pltpu.VMEM((n_mp, 2 * head_size, feature), bf16),
             pltpu.VMEM((feature, feature), bf16),
@@ -908,16 +1028,19 @@
             pltpu.VMEM((seq_span, 4 * LANES), bf16),
             pltpu.VMEM((2, 2, seq_span, 2 * LANES), bf16),
             pltpu.VMEM((2 * masks, 4 * LANES), bf16),
+            pltpu.VMEM((n_mp, 2 * masks, LANES), bf16),
+            pltpu.VMEM((n_mp, 2 * masks, LANES), bf16),
             pltpu.VMEM((2 * masks, feature), f32),
             pltpu.VMEM((masks, feature), f32),
             pltpu.VMEM((devices, 8, LANES), f32),
             dma((7,)),
-            dma((32,)),
-            dma((n_mp, 8)),
+            dma((64,)),
+            dma((n_mp, 16)),
+            dma((2, n_mp)),
             dma((tiles,)),
             dma((tiles,)),
-            dma((2,)),
-            dma((2,)),
+            dma((4,)),
+            dma((4,)),
             dma((devices,)),
             dma((devices,)),
             pltpu.SemaphoreType.REGULAR((5,)),

time: 58.9 us -> 51.9 us (0.88)
  Pallas kernels: 55.4 us -> 48.4 us
    pallas_call x1, Pallas kernels: 55.4 us -> 48.4 us  [split_call(): pl.pallas_call(functools.partial(split_kernel, (n_dp, n_mp, head_size)),...]
where the time goes in v2:
time: 51.9 us; the launch traced here: 51.7 us
  Pallas kernels  48.4 us (93%)
  local copies, waits for them, and re-layouts  3.27 us (6%)
    pallas_call x1, Pallas kernels, split_call(): pl.pallas_call(functools.partial(split_kernel, (n_dp, n_mp, head_size)),...  48.4 us
    transpose x1, local copies, waits for them, and re-layouts, on_device(): jnp.swapaxes(output_weight, 0, 1).reshape(heads * head_size, feature)  1.99 us
    dynamic_slice x1, local copies, waits for them, and re-layouts, on_device(): return lax.dynamic_slice_in_dim(rows, lax.axis_index('mp') * own, own, 1)  1.29 us

profile of v2, /device:TPU:0, one launch (start us, length us, event | category | flops | bytes accessed | tf_op | source)
XLA Modules:
  0.0 51.7 jit_solution(14334537382178310143)
XLA Ops:
  0.0 2.0 %copy.17 = bf16[4,64,1280]{2,1,0:T(8,128)(2,1)} copy(bf16[4,64,1280]{2,0,1:T(4,128)(2,1)} %bitcast.12) | data formatting | bytes 1310720 | tf_op jit(solution)/shard_map/transpose | solution.py:1088
  2.0 48.4 %score_split.1 = f32[4,128]{1,0:T(4,128)} custom-call(s32[32]{0:T(128)} %sequence_ref.1, s32[24]{0:T(128)} %lengths_ref.1, s32[32,64]{1,0:T(8,128)} %codes_ref.1, s32[24,640]{1,0:T(8,128)} %tokens_ref.1, s32[1,32]{1,0:T(1,128)} %bitcast.14, f32[1280]{0:T(1024)} %gain_ref.1, f32[1280]{0:T(1024)} %final_gain_ref.1, bf16[33,1280]{1,0:T(8,128)(2,1)} %bitcast.13, ...), custom_call_target="tpu_custom_call" | custom-call | tf_op jit(solution)/shard_map/score_split/pallas_call | solution.py:1013
  50.4 1.3 %constant_dynamic-slice_fusion = f32[4,16]{1,0:T(4,128)} fusion(f32[4,128]{1,0:T(4,128)} %score_split.1, s32[]{:T(128)S(6)} %select_n.3), kind=kLoop, calls=%fused_computation | loop fusion | bytes 516 | tf_op jit(solution)/shard_map/dynamic_slice | solution.py:1111

commit v3 on v2

--- a/solution.py
+++ b/solution.py
@@ -438,8 +438,10 @@
 
 ITEMS = {"K0": 0, "V0": 1, "K1": 2, "V1": 3, "Q0": 4, "Q1": 5, "O0": 6, "O1": 7}
 FIRST_ROW = {"Q": 0, "K": 64, "V": 128}
-ENDS = [('0V0.1>xy', '0V0.0>xy', '0K0.1>xy', '0O0.0>y', '0O0.1>x'),
- ('0K0.0>xy',
+ENDS = [('0V0.1>xy', '0V0.0>xy', '0K0.1>xy'),
+ ('0O0.0>y',
+  '0O0.1>x',
+  '0K0.0>xy',
   '0R',
   '2V0.1>e',
   '1K0.1>e',
@@ -463,8 +465,9 @@
  ('2O1.1', '1O0.0'),
  ('3G', '1O1.1', '3O1.1'),
  ('3O1.0',)]
-MIDS = [('0ox.1>y', '0V1.0>x', '0qx.1>y', '0K1.1>x', '0K1.0>x'),
- ('0V1.0>y',
+MIDS = [('0V1.0>x', '0qx.1>y', '0K1.1>x', '0K1.0>x'),
+ ('0ox.1>y',
+  '0V1.0>y',
   '0K1.0>y',
   '0qx.1>x',
   '0qx.0>x',
@@ -507,6 +510,23 @@
 
 def split_kernel(
     sizes,
+    sequence_hbm,
+    lengths_hbm,
+    codes_hbm,
+    tokens_hbm,
+    owner_hbm,
+    gain_hbm,
+    final_gain_hbm,
+    decoder_hbm,
+    bias_hbm,
+    hidden_hbm,
+    weight_hbm,
+    out_weight_hbm,
+    dense_hbm,
+    cos_hbm,
+    sin_hbm,
+    split_hbm,
+    out_ref,
     sequence_ref,
     lengths_ref,
     codes_ref,
@@ -516,18 +536,11 @@
     final_gain_ref,
     decoder_ref,
     bias_ref,
-    hidden_hbm,
-    weight_hbm,
-    out_weight_hbm,
-    dense_hbm,
-    cos_hbm,
-    sin_hbm,
-    split_hbm,
-    out_ref,
     hidden,
     normed,
     rows_buf,
     wbuf,
+    raw,
     obuf,
     dense,
     cos,
@@ -591,9 +604,31 @@
         return copy
 
     weight_copy = local(1, weight_hbm.at[core], wbuf.at[0])
-    out_start = pl.multiple_of(core * 2 * head_size, 2 * head_size)
-    out_weight_copy = local(2, out_weight_hbm.at[pl.ds(out_start, 2 * head_size), :], obuf.at[0])
     hidden_copy = local(0, hidden_hbm, hidden)
+    small_copies = [
+        local(7 + place, source, target)
+        for place, (source, target) in enumerate(
+            (
+                (sequence_hbm, sequence_ref),
+                (lengths_hbm, lengths_ref),
+                (codes_hbm, codes_ref),
+                (tokens_hbm, tokens_ref),
+                (gain_hbm, gain_ref),
+            )
+        )
+    ]
+    out_weight_copy = local(2, out_weight_hbm.at[:, pl.ds(pl.multiple_of(2 * core, 2), 2), :], raw)
+    late_copies = [
+        local(12 + place, source, target)
+        for place, (source, target) in enumerate(
+            (
+                (owner_hbm, owner_ref),
+                (final_gain_hbm, final_gain_ref),
+                (decoder_hbm, decoder_ref),
+                (bias_hbm, bias_ref),
+            )
+        )
+    ]
     cos_copy = local(3, cos_hbm, cos)
     sin_copy = local(4, sin_hbm, sin)
     split_copy = local(6, split_hbm, split)
@@ -694,9 +729,13 @@
                 serve(ENDS[index], False)
 
     weight_copy.wait()
-    out_weight_copy.wait()
     pl.semaphore_wait(barrier, 4 + middle.astype(jnp.int32))
     service(0)
+    for copy in small_copies:
+        copy.wait()
+    out_weight_copy.wait()
+    for head in range(2):
+        obuf[0, head * head_size : (head + 1) * head_size, :] = raw[:, head, :]
     signal(token_sem.at[0], (partner, mp))
 
     def tokens_step(step):
@@ -927,6 +966,8 @@
     )
     inbox_copy.start()
     dense_copy.wait()
+    for copy in late_copies:
+        copy.wait()
     for step in range(seq_span // tile):
         norm_copy(step).wait_send()
     rows_copy(0, 1, "d", 0).wait_send()
@@ -960,36 +1001,25 @@
     scores[me] = jnp.broadcast_to(padded, scores.shape[1:])
 
     def score_copy(step):
-        other = (me + step) % devices
+        other_dp, other_mp = flip(dp, step // n_mp), flip(mp, step % n_mp)
         return pltpu.make_async_remote_copy(
             src_ref=scores.at[me, pl.ds(0, 1), :],
             dst_ref=scores.at[me, pl.ds(0, 1), :],
             send_sem=score_send_sem.at[step],
-            recv_sem=score_sem.at[me],
-            device_id=(other // n_mp, other % n_mp),
+            recv_sem=score_sem.at[step],
+            device_id=(other_dp, other_mp),
             device_id_type=MESH,
         )
 
-    def send_scores(step, carry):
+    for step in reversed(range(1, devices)):
         score_copy(step).start()
-        return carry
-
-    lax.fori_loop(1, devices, send_scores, 0)
     inbox_copy.wait_send()
-
-    def wait_scores(step, carry):
-        source = (me + step) % devices
+    for step in range(1, devices):
+        source = flip(dp, step // n_mp) * n_mp + flip(mp, step % n_mp)
         landing = scores.at[source, pl.ds(0, 1), :]
-        pltpu.make_async_copy(landing, landing, score_sem.at[source]).wait()
-        return carry
-
-    lax.fori_loop(1, devices, wait_scores, 0)
-
-    def wait_sends(step, carry):
+        pltpu.make_async_copy(landing, landing, score_sem.at[step]).wait()
+    for step in range(1, devices):
         score_copy(step).wait_send()
-        return carry
-
-    lax.fori_loop(1, devices, wait_sends, 0)
     group = out_ref.shape[0]
     wanted = dp * group + lax.broadcasted_iota(jnp.int32, (group, owner_ref.shape[1]), 0)
     select = jnp.where(owner_ref[...] == wanted, 1.0, 0.0)
@@ -1007,20 +1037,21 @@
     split = np.concatenate(parts, axis=1).astype(jnp.bfloat16)
     dma = pltpu.SemaphoreType.DMA
     vmem = pl.BlockSpec(memory_space=pltpu.VMEM)
-    smem = pl.BlockSpec(memory_space=pltpu.SMEM)
     anywhere = pl.BlockSpec(memory_space=pl.ANY)
     tiles = seq_span // 128
     return pl.pallas_call(
         functools.partial(split_kernel, (n_dp, n_mp, head_size)),
         name="score_split",
         out_shape=jax.ShapeDtypeStruct((group, LANES), f32),
-        in_specs=[smem] * 2 + [vmem] * 7 + [anywhere] * 7,
+        in_specs=[anywhere] * 16,
         out_specs=vmem,
-        scratch_shapes=[
+        scratch_shapes=[(pltpu.SMEM if place < 2 else pltpu.VMEM)(x.shape, x.dtype) for place, x in enumerate(inputs)]
+        + [
             pltpu.VMEM((seq_span, feature), bf16),
             pltpu.VMEM((2, seq_span, feature), bf16),
             pltpu.VMEM((4, masks, feature), bf16),
             pltpu.VMEM((n_mp, width, feature), bf16),
+            pltpu.VMEM((head_size, 2, feature), bf16),
             pltpu.VMEM((n_mp, 2 * head_size, feature), bf16),
             pltpu.VMEM((feature, feature), bf16),
             pltpu.VMEM((seq_span, LANES), f32),
@@ -1033,7 +1064,7 @@
             pltpu.VMEM((2 * masks, feature), f32),
             pltpu.VMEM((masks, feature), f32),
             pltpu.VMEM((devices, 8, LANES), f32),
-            dma((7,)),
+            dma((16,)),
             dma((64,)),
             dma((n_mp, 16)),
             dma((2, n_mp)),
@@ -1085,7 +1116,6 @@
     chunks = heads // in_chunk
     width = in_chunk * 3 * head_size
     weight = jnp.transpose(w_qkv.reshape(feature, chunks, width), (1, 2, 0))
-    out_weight = jnp.swapaxes(output_weight, 0, 1).reshape(heads * head_size, feature)
     cosine, sine = rotary_tables(seq_span, head_size)
     group = copies // n_dp
     items = 2 * chunks + 2
@@ -1107,8 +1137,9 @@
     )
     if n_mp == 4 and n_dp == 8 and heads == 4 and seq_span % 128 == 0:
         hidden = hidden_states.reshape(seq_span, feature)
-        rows = split_call(shape, inputs, weight, out_weight, hidden, dense_weight, cosine, sine, group, head_size)
+        rows = split_call(shape, inputs, weight, output_weight, hidden, dense_weight, cosine, sine, group, head_size)
         return lax.dynamic_slice_in_dim(rows, lax.axis_index("mp") * own, own, 1)
+    out_weight = jnp.swapaxes(output_weight, 0, 1).reshape(heads * head_size, feature)
     rows = pl.pallas_call(
         functools.partial(kernel, (n_dp, n_mp, head_size, in_chunk, chunks)),
         name="score_copies",

time: 51.9 us -> 49.9 us (0.961)
  local copies, waits for them, and re-layouts: 3.27 us -> 1.34 us
    transpose x1 -> x0, local copies, waits for them, and re-layouts: 1.99 us -> none  [on_device(): jnp.swapaxes(output_weight, 0, 1).reshape(heads * head_size, feature)]
where the time goes in v3:
time: 49.9 us; the launch traced here: 49.7 us
  Pallas kernels  48.4 us (97%)
  local copies, waits for them, and re-layouts  1.34 us (3%)
    pallas_call x1, Pallas kernels, split_call(): pl.pallas_call(functools.partial(split_kernel, (n_dp, n_mp, head_size)),...  48.4 us
    dynamic_slice x1, local copies, waits for them, and re-layouts, on_device(): return lax.dynamic_slice_in_dim(rows, lax.axis_index('mp') * own, own, 1)  1.34 us

profile of v3, /device:TPU:0, one launch (start us, length us, event | category | flops | bytes accessed | tf_op | source)
XLA Modules:
  0.0 49.7 jit_solution(10011379464780586148)
XLA Ops:
  0.0 48.4 %score_split.1 = f32[4,128]{1,0:T(4,128)} custom-call(s32[32]{0:T(128)} %sequence_hbm.1, s32[24]{0:T(128)} %lengths_hbm.1, s32[32,64]{1,0:T(8,128)} %codes_hbm.1, s32[24,640]{1,0:T(8,128)} %tokens_hbm.1, s32[1,32]{1,0:T(1,128)} %bitcast.10, f32[1280]{0:T(1024)} %gain_hbm.1, f32[1280]{0:T(1024)} %final_gain_hbm.1, bf16[33,1280]{1,0:T(8,128)(2,1)} %bitcast.9, ...), custom_call_target="tpu_custom_call" | custom-call | tf_op jit(solution)/shard_map/score_split/pallas_call | solution.py:1042
  48.4 1.3 %constant_dynamic-slice_fusion = f32[4,16]{1,0:T(4,128)} fusion(f32[4,128]{1,0:T(4,128)} %score_split.1, s32[]{:T(128)S(6)} %select_n.3), kind=kLoop, calls=%fused_computation | loop fusion | bytes 516 | tf_op jit(solution)/shard_map/dynamic_slice | solution.py:1141

commit v4 on v3

--- a/solution.py
+++ b/solution.py
@@ -436,76 +436,33 @@
     out_ref[...] = jnp.dot(select, scores[:, 0, :], **exact)
 
 
-ITEMS = {"K0": 0, "V0": 1, "K1": 2, "V1": 3, "Q0": 4, "Q1": 5, "O0": 6, "O1": 7}
-FIRST_ROW = {"Q": 0, "K": 64, "V": 128}
-ENDS = [('0V0.1>xy', '0V0.0>xy', '0K0.1>xy'),
- ('0O0.0>y',
-  '0O0.1>x',
-  '0K0.0>xy',
-  '0R',
-  '2V0.1>e',
-  '1K0.1>e',
-  '2O0.0>x',
-  '0O0.1>y',
-  '1V0.1>ey',
-  '2K0.0>ex',
-  '3V0.1',
-  '0O1.0>xy',
-  '1V0.0>ey'),
- ('1K0.0>e', '0O0.0>x'),
- ('1K1.1>y', '1O0.1', '1O1.0', '2K0.1>ex', '1K1.0>y'),
- ('1V1.0', '2O0.1>x'),
- ('2V1.0', '2V0.0>e'),
- ('2K1.0', '3K0.0>e', '3K0.1>e'),
- ('2G', '0O1.1>xy', '2V1.1', '1G', '3V0.0'),
- ('3O0.1>e', '3K1.1', '2K1.1', '1V1.1'),
- (),
- ('2O1.0', '3V1.1', '3K1.0'),
- ('3V1.0', '3O0.0>e'),
- ('2O1.1', '1O0.0'),
- ('3G', '1O1.1', '3O1.1'),
- ('3O1.0',)]
-MIDS = [('0V1.0>x', '0qx.1>y', '0K1.1>x', '0K1.0>x'),
- ('0ox.1>y',
-  '0V1.0>y',
-  '0K1.0>y',
-  '0qx.1>x',
-  '0qx.0>x',
-  '1V1.0>e',
-  '2ox.1>m',
-  '1K1.1>e',
-  '0V1.1>y',
-  '0qx.0>y',
-  '2qx.1>m',
-  '2V1.0>ex',
-  '0V1.1>x',
-  '0ox.0>x',
-  '0ox.0>y'),
- ('9R', '1K1.0>e', '1qx.1>my', '1qx.0>my', '2oy.1', '2O1!1>x', '2K1.0>e', '2V1.1>ex'),
- (),
- ('2qx.0>m', '2ox.0>m', '1V1.1>e', '3V1.0>e', '2K0.0', '1V0.1', '0ox.1>x', '2qy.1', '0K1.1>y'),
- ('3qx.1>m',
-  '1qy.1',
-  '2V0.1',
-  '1qy.0',
-  'q1',
-  '2qy.0',
-  '1V0.0',
-  '3qx.0>m',
-  '1kx!1>y',
-  'q2',
-  '1kx!0>y',
-  '2K1.1>e',
-  '1ox.0>m'),
- ('3V1.1>e',),
- ('1K0.1', '3kx.1>m', '2oy.0', '2O1!0>x', '3O1.1>e', '3qy.0', '3qy.1'),
- ('q3', '3kx.0>m', '2V0.0', '1ox.1>m', '2K0.1', '1K0.0'),
- (),
- ('3O1.0>e', '3K0.0', '3ky.1'),
- ('3K0.1', '3ky.0', '1oy.0'),
- (),
- (),
- ('1oy.1', '3O0.0', '3O0.1')]
+FIRST_ROW = (1, 2, 4, 5, 0, 3, 0, 1)
+WAIT, ROWS, QUERY = 1024, 2048, 2052
+PLANS = (((133, 194, 128, 69), (79, 1058, 140, 68, 1301, 70), (2048, 142, 290),
+  (131, 1061, 64, 1068, 1044, 1057, 293, 1055, 77, 108, 148, 143, 159), (),
+  (98, 287, 1059, 1084, 1076, 1326, 1040, 110, 316, 134, 1047, 1043, 1056, 1071, 144, 1041, 1053, 145, 300,
+   76, 151, 1062, 1046, 102, 1042, 285),
+  (), (308, 2050, 1074, 99, 1072, 1060, 149, 2049, 157, 1052), (1063,), (), (1079, 1069, 1086, 284, 1078),
+  (1073, 1077, 1075), (), (1087, 2051, 1054), (1085,)),
+ ((129, 71, 68, 137, 135, 132), (1057, 1047, 141, 535, 73, 67), (72, 134, 65, 1044, 1065, 66, 553, 801),
+  (1060, 1045, 1049, 292, 128, 537, 1063, 1043), (1064, 533, 275, 131),
+  (279, 74, 103, 1041, 105, 273, 147, 807, 548, 531, 1069, 145, 1046, 1125, 1075, 1050, 2048, 1058, 1051,
+   1067, 1048, 563, 1168, 1079, 1066, 2053, 106, 1056, 155, 1055, 2054, 301, 1073, 98, 1042, 1062, 530, 102),
+  (), (1059,), (1080, 1071, 1054), (1580, 1084, 1083, 1082, 1081, 1072, 1077, 1053, 557, 111, 414, 2055),
+  (1070,), (1076, 1074, 1078, 1085), (), (1086, 1087, 1052), ()),
+ ((128, 70, 136, 68), (75, 1302, 138, 77, 74, 534, 1064, 139, 1044, 104, 143, 552, 1040, 148, 528),
+  (1051, 1067, 72, 555, 1053, 134, 276, 150, 1066, 285, 78, 539, 1047), (1065, 279, 554), (1076, 1057),
+  (1592, 106, 1050, 289, 151, 1071, 157, 79, 1058, 2048, 303, 155, 1062, 559, 1063, 1054, 1048, 144, 1041,
+   1049, 2053, 2054, 105, 1173, 1061, 1060, 542, 1082, 286),
+  (308,), (1043,), (1042, 1085, 1059, 1055, 1081, 573, 1075, 97, 1070, 1083, 2055, 1056),
+  (110, 159, 1072, 1074, 1079), (), (1073, 1078, 1077), (), (1086, 1052, 1084, 1068), (1069, 1087)),
+ ((131, 64, 130, 67),
+  (128, 1040, 133, 76, 272, 65, 1058, 1059, 142, 1056, 99, 134, 98, 1046, 66, 141, 2048, 132, 79, 290, 1061,
+   1041),
+  (1052, 273), (293,), (1070, 156, 135), (101, 96, 1042, 1074, 1053, 140, 302, 291, 1043, 69, 1084, 1057),
+  (1071, 150, 1044, 110, 306, 1047), (1060, 1062, 2050, 284, 97, 2049, 151), (1045, 1075, 1063), (),
+  (1077, 1072, 1069, 157, 111, 316), (2051, 1055, 1079, 1078, 1073, 1076), (), (),
+  (1068, 1054, 1087, 1085, 1086)))
 
 
 def split_kernel(
@@ -557,11 +514,9 @@
     send_sem,
     arrive_sem,
     query_sem,
-    norm_send_sem,
     norm_sem,
     swap_send_sem,
     swap_sem,
-    score_send_sem,
     score_sem,
     token_sem,
 ):
@@ -579,7 +534,6 @@
     pair = dp + 2 - 4 * parity
     twin = dp - 2 + 4 * parity
     middle = jnp.logical_and(layer > 0, layer < layers - 1)
-    side = 1 - parity
     seq_span, feature = hidden.shape
     masks = codes_ref.shape[1]
     head_rows = 3 * head_size
@@ -634,23 +588,9 @@
     split_copy = local(6, split_hbm, split)
     dense_copy = local(5, dense_hbm, dense)
 
-    def number(item):
-        if item in ITEMS:
-            return ITEMS[item]
-        return {"qx": 4 + side, "qy": 5 - side, "ox": 6 + side, "oy": 7 - side, "kx": 2 - side, "ky": 1 + side}[item]
-
     def view(relation, item, half):
-        if item in ITEMS:
-            kind, head = item[0], int(item[1])
-            start = head * head_size if kind == "O" else head * head_rows + FIRST_ROW[kind]
-        elif item[0] == "k":
-            kind = "K"
-            start = 256 - 128 * side if item == "kx" else 128 + 128 * side
-        else:
-            kind = item[0].upper()
-            start = (side if item[1] == "x" else 1 - side) * (head_rows if kind == "Q" else head_size)
-        rows = pl.ds(pl.multiple_of(start + half * half_rows, half_rows), half_rows)
-        return (obuf if kind == "O" else wbuf).at[relation, rows, :]
+        start = FIRST_ROW[item] * head_size
+        return (obuf if item > 5 else wbuf).at[relation, pl.ds(start + half * half_rows, half_rows), :]
 
     flips = {"x": 1, "y": 2, "e": 0, "m": 0}
 
@@ -659,8 +599,8 @@
         return pltpu.make_async_remote_copy(
             src_ref=view(relation, item, half),
             dst_ref=view(target, item, half),
-            send_sem=send_sem.at[index],
-            recv_sem=arrive_sem.at[target, 2 * number(item) + half],
+            send_sem=send_sem.at[index // 12],
+            recv_sem=arrive_sem.at[target - 1, 2 * item + half],
             device_id=where[link],
             device_id_type=MESH,
         )
@@ -679,54 +619,44 @@
         return pltpu.make_async_remote_copy(
             src_ref=gbuf.at[relation],
             dst_ref=qbuf.at[relation],
-            send_sem=query_sem.at[0, relation],
-            recv_sem=query_sem.at[1, relation],
+            send_sem=query_sem.at[0, relation - 1],
+            recv_sem=query_sem.at[1, relation - 1],
             device_id=where["e"],
             device_id_type=MESH,
         )
 
-    sent = {True: [], False: []}
-
-    def serve(words, in_middle):
+    sent = [[] for _ in range(layers)]
+
+    def serve(words, place):
+        inner = 0 < place < layers - 1
         for word in words:
-            if word in ("q1", "q2", "q3"):
-                project_queries(int(word[1]))
-                continue
-            name, _, links = word.partition(">")
-            relation, item = int(name[0]), name[1:3]
-            if item == "R":
-                if in_middle:
-                    rows_copy(0, 2, "e", 1).wait_recv()
-                    rows_copy(2, 3, "d", 2).start()
-                else:
-                    rows_copy(0, 2, "e", 1).start()
-                continue
-            if item == "G":
-                query_copy(relation).wait_recv()
-                continue
-            half = int(name[4])
-            if relation and name[3] != "!":
-                landing = view(relation, item, half)
-                pltpu.make_async_copy(
-                    landing, landing, arrive_sem.at[relation, 2 * number(item) + half]
-                ).wait()
-            for link in links:
-                index = len(sent[in_middle])
-                sent[in_middle].append((relation, item, half, link, index))
-                piece_copy(relation, item, half, link, index).start()
+            if word > QUERY:
+                project_queries(word - QUERY)
+            elif word > ROWS:
+                query_copy(word - ROWS).wait_recv()
+            elif word == ROWS and inner:
+                rows_copy(0, 2, "e", 1).wait_recv()
+                rows_copy(2, 3, "d", 2).start()
+            elif word == ROWS:
+                rows_copy(0, 2, "e", 1).start()
+            else:
+                relation, item, half = word // 16 % 4, word // 2 % 8, word % 2
+                if word >= WAIT:
+                    landing = view(relation, item, half)
+                    pltpu.make_async_copy(landing, landing, arrive_sem.at[relation - 1, 2 * item + half]).wait()
+                for place_of, link in enumerate("xyem"):
+                    if word // 64 % 16 & (1 << place_of):
+                        record = (relation, item, half, link, len(sent[place]))
+                        sent[place].append(record)
+                        piece_copy(*record).start()
 
     def service(index):
-        if MIDS[index]:
-
-            @pl.when(middle)
-            def _():
-                serve(MIDS[index], True)
-
-        if ENDS[index]:
-
-            @pl.when(jnp.logical_not(middle))
-            def _():
-                serve(ENDS[index], False)
+        for place in range(layers):
+            if PLANS[place][index]:
+
+                @pl.when(layer == place)
+                def _():
+                    serve(PLANS[place][index], place)
 
     weight_copy.wait()
     pl.semaphore_wait(barrier, 4 + middle.astype(jnp.int32))
@@ -796,16 +726,14 @@
     hidden_copy.wait()
     tile = 128
 
-    def norm_copy(step):
-        rows = pl.ds(pl.multiple_of(step * tile, tile), tile)
-        return pltpu.make_async_remote_copy(
-            src_ref=normed.at[0, rows, :],
-            dst_ref=normed.at[1, rows, :],
-            send_sem=norm_send_sem.at[step],
-            recv_sem=norm_sem.at[step],
-            device_id=(partner, mp),
-            device_id_type=MESH,
-        )
+    norm_copy = pltpu.make_async_remote_copy(
+        src_ref=normed.at[0],
+        dst_ref=normed.at[1],
+        send_sem=norm_sem.at[0],
+        recv_sem=norm_sem.at[1],
+        device_id=(partner, mp),
+        device_id_type=MESH,
+    )
 
     def norm_rows(step, carry):
         rows = pl.ds(pl.multiple_of(step * tile, tile), tile)
@@ -814,8 +742,7 @@
 
     lax.fori_loop(0, seq_span // tile, norm_rows, 0)
     rows_buf[0] = jnp.dot(onehot, normed[0], preferred_element_type=f32).astype(bf16)
-    for step in range(seq_span // tile):
-        norm_copy(step).start()
+    norm_copy.start()
     mixed[:masks, :] = jnp.dot(onehot, hidden[...], preferred_element_type=f32)
     mixed[masks:, :] = jnp.zeros((masks, feature), f32)
     rows_copy(0, 1, "d", 0).start()
@@ -836,7 +763,7 @@
         )
         return inputs * cosine + turned * sine
 
-    span = seq_span // 2
+    span = seq_span
 
     def stack(refs):
         return jnp.concatenate([ref[...] for ref in refs], axis=0)
@@ -923,8 +850,7 @@
     attend(0, 0, 0, of_head(query, 0), of_head(query, 1))
     tokens_step(0)
     service(3)
-    for step in range(seq_span // tile):
-        norm_copy(step).wait_recv()
+    norm_copy.wait_recv()
     rows_copy(0, 1, "d", 0).wait_recv()
     project(own, 0, 1)
     service(4)
@@ -968,24 +894,6 @@
     dense_copy.wait()
     for copy in late_copies:
         copy.wait()
-    for step in range(seq_span // tile):
-        norm_copy(step).wait_send()
-    rows_copy(0, 1, "d", 0).wait_send()
-
-    @pl.when(middle)
-    def _():
-        for record in sent[True]:
-            piece_copy(*record).wait_send()
-        rows_copy(2, 3, "d", 2).wait_send()
-        for relation in (1, 2, 3):
-            query_copy(relation).wait_send()
-
-    @pl.when(jnp.logical_not(middle))
-    def _():
-        for record in sent[False]:
-            piece_copy(*record).wait_send()
-        rows_copy(0, 2, "e", 1).wait_send()
-
     inbox_copy.wait_recv()
     residual = mixed[:masks, :] + inbox[...]
     normed_final = (layer_norm(residual) * final_gain_ref[...].reshape(1, feature)).astype(bf16)
@@ -997,16 +905,16 @@
     vocabulary = lax.broadcasted_iota(jnp.int32, logits.shape, 1).astype(f32)
     picked = jnp.sum(jnp.where(vocabulary == targets, logits - scale, 0.0), axis=1, keepdims=True)
     row = jnp.sum(jnp.where(eye, picked, 0.0), axis=0, keepdims=True)
-    padded = jnp.pad(row, ((0, 0), (0, LANES - masks)))
-    scores[me] = jnp.broadcast_to(padded, scores.shape[1:])
+    padded = jnp.concatenate([row] * (LANES // masks), axis=1)
+    scores[me] = padded
 
     def score_copy(step):
         other_dp, other_mp = flip(dp, step // n_mp), flip(mp, step % n_mp)
         return pltpu.make_async_remote_copy(
-            src_ref=scores.at[me, pl.ds(0, 1), :],
-            dst_ref=scores.at[me, pl.ds(0, 1), :],
-            send_sem=score_send_sem.at[step],
-            recv_sem=score_sem.at[step],
+            src_ref=scores.at[me],
+            dst_ref=scores.at[me],
+            send_sem=score_sem.at[0],
+            recv_sem=score_sem.at[1],
             device_id=(other_dp, other_mp),
             device_id_type=MESH,
         )
@@ -1014,16 +922,36 @@
     for step in reversed(range(1, devices)):
         score_copy(step).start()
     inbox_copy.wait_send()
-    for step in range(1, devices):
-        source = flip(dp, step // n_mp) * n_mp + flip(mp, step % n_mp)
-        landing = scores.at[source, pl.ds(0, 1), :]
-        pltpu.make_async_copy(landing, landing, score_sem.at[step]).wait()
-    for step in range(1, devices):
-        score_copy(step).wait_send()
+    norm_copy.wait_send()
+    rows_copy(0, 1, "d", 0).wait_send()
+
+    for place in range(layers):
+
+        @pl.when(layer == place)
+        def _():
+            for group in range(0, len(sent[place]), 12):
+                count = min(12, len(sent[place]) - group)
+                bulk = wbuf.at[0, pl.ds(0, count * half_rows), :]
+                pltpu.make_async_copy(bulk, bulk, send_sem.at[group // 12]).wait()
+            if 0 < place < layers - 1:
+                rows_copy(2, 3, "d", 2).wait_send()
+                for relation in (1, 2, 3):
+                    query_copy(relation).wait_send()
+            else:
+                rows_copy(0, 2, "e", 1).wait_send()
+
     group = out_ref.shape[0]
-    wanted = dp * group + lax.broadcasted_iota(jnp.int32, (group, owner_ref.shape[1]), 0)
-    select = jnp.where(owner_ref[...] == wanted, 1.0, 0.0)
-    out_ref[...] = jnp.dot(select, scores[:, 0, :], preferred_element_type=f32, precision=lax.Precision.HIGHEST)
+    square = lax.broadcasted_iota(jnp.int32, (devices, devices), 0) == lax.broadcasted_iota(
+        jnp.int32, (devices, devices), 1
+    )
+    owners = jnp.sum(jnp.where(square, owner_ref[...].astype(f32), 0.0), axis=1, keepdims=True)
+    selects = [jnp.where(owners == (dp * group + place).astype(f32), 1.0, 0.0) for place in range(group)]
+    everyone = scores.at[pl.ds(0, devices - 1)]
+    pltpu.make_async_copy(everyone, everyone, score_sem.at[1]).wait()
+    pltpu.make_async_copy(everyone, everyone, score_sem.at[0]).wait()
+    gathered = scores[...].reshape(devices, LANES)
+    result = jnp.concatenate([jnp.sum(gathered * select, axis=0, keepdims=True) for select in selects], axis=0)
+    out_ref[...] = pltpu.roll(result, LANES - mp * out_ref.shape[1], 1)[:, : out_ref.shape[1]]
 
 
 def split_call(shape, inputs, weight, out_weight, hidden, dense_weight, cosine, sine, group, head_size):
@@ -1038,11 +966,10 @@
     dma = pltpu.SemaphoreType.DMA
     vmem = pl.BlockSpec(memory_space=pltpu.VMEM)
     anywhere = pl.BlockSpec(memory_space=pl.ANY)
-    tiles = seq_span // 128
     return pl.pallas_call(
         functools.partial(split_kernel, (n_dp, n_mp, head_size)),
         name="score_split",
-        out_shape=jax.ShapeDtypeStruct((group, LANES), f32),
+        out_shape=jax.ShapeDtypeStruct((group, masks // n_mp), f32),
         in_specs=[anywhere] * 16,
         out_specs=vmem,
         scratch_shapes=[(pltpu.SMEM if place < 2 else pltpu.VMEM)(x.shape, x.dtype) for place, x in enumerate(inputs)]
@@ -1063,17 +990,15 @@
             pltpu.VMEM((n_mp, 2 * masks, LANES), bf16),
             pltpu.VMEM((2 * masks, feature), f32),
             pltpu.VMEM((masks, feature), f32),
-            pltpu.VMEM((devices, 8, LANES), f32),
+            pltpu.VMEM((devices, 1, LANES), f32),
             dma((16,)),
-            dma((64,)),
-            dma((n_mp, 16)),
-            dma((2, n_mp)),
-            dma((tiles,)),
-            dma((tiles,)),
+            dma((6,)),
+            dma((n_mp - 1, 16)),
+            dma((2, n_mp - 1)),
+            dma((2,)),
             dma((4,)),
             dma((4,)),
-            dma((devices,)),
-            dma((devices,)),
+            dma((2,)),
             pltpu.SemaphoreType.REGULAR((5,)),
         ],
         compiler_params=pltpu.CompilerParams(collective_id=1, has_side_effects=True),
@@ -1137,8 +1062,7 @@
     )
     if n_mp == 4 and n_dp == 8 and heads == 4 and seq_span % 128 == 0:
         hidden = hidden_states.reshape(seq_span, feature)
-        rows = split_call(shape, inputs, weight, output_weight, hidden, dense_weight, cosine, sine, group, head_size)
-        return lax.dynamic_slice_in_dim(rows, lax.axis_index("mp") * own, own, 1)
+        return split_call(shape, inputs, weight, output_weight, hidden, dense_weight, cosine, sine, group, head_size)
     out_weight = jnp.swapaxes(output_weight, 0, 1).reshape(heads * head_size, feature)
     rows = pl.pallas_call(
         functools.partial(kernel, (n_dp, n_mp, head_size, in_chunk, chunks)),

time: 49.9 us -> 45.6 us (0.914)
  Pallas kernels: 48.4 us -> 44.2 us
    pallas_call x1, Pallas kernels: 48.4 us -> 44.2 us  [split_call(): pl.pallas_call(functools.partial(split_kernel, (n_dp, n_mp, head_size)),...]
    dynamic_slice x1 -> x0, local copies, waits for them, and re-layouts: 1.34 us -> none  [on_device(): return lax.dynamic_slice_in_dim(rows, lax.axis_index('mp') * own, own, 1)]
    unnamed x0 -> x1, local copies, waits for them, and re-layouts: none -> 1.26 us
where the time goes in v4:
time: 45.6 us; the launch traced here: 45.4 us
  Pallas kernels  44.2 us (97%)
  local copies, waits for them, and re-layouts  1.26 us (3%)
    pallas_call x1, Pallas kernels, split_call(): pl.pallas_call(functools.partial(split_kernel, (n_dp, n_mp, head_size)),...  44.2 us
    unnamed x1, local copies, waits for them, and re-layouts  1.26 us

profile of v4, /device:TPU:0, one launch (start us, length us, event | category | flops | bytes accessed | tf_op | source)
XLA Modules:
  0.0 45.4 jit_solution(4517006855451996218)
XLA Ops:
  0.0 44.2 %score_split.1 = f32[4,16]{1,0:T(4,128)} custom-call(s32[32]{0:T(128)} %sequence_hbm.1, s32[24]{0:T(128)} %lengths_hbm.1, s32[32,64]{1,0:T(8,128)} %codes_hbm.1, s32[24,640]{1,0:T(8,128)} %tokens_hbm.1, s32[1,32]{1,0:T(1,128)} %bitcast.10, f32[1280]{0:T(1024)} %gain_hbm.1, f32[1280]{0:T(1024)} %final_gain_hbm.1, bf16[33,1280]{1,0:T(8,128)(2,1)} %bitcast.9, ...), custom_call_target="tpu_custom_call" | custom-call | tf_op jit(solution)/shard_map/score_split/pallas_call | solution.py:969
  44.2 1.3 %copy.18 = f32[4,16]{1,0:T(4,128)} copy(f32[4,16]{1,0:T(4,128)} %score_split.1) | data formatting | bytes 512

commit v5 on v4

--- a/solution.py
+++ b/solution.py
@@ -438,31 +438,31 @@
 
 FIRST_ROW = (1, 2, 4, 5, 0, 3, 0, 1)
 WAIT, ROWS, QUERY = 1024, 2048, 2052
-PLANS = (((133, 194, 128, 69), (79, 1058, 140, 68, 1301, 70), (2048, 142, 290),
-  (131, 1061, 64, 1068, 1044, 1057, 293, 1055, 77, 108, 148, 143, 159), (),
-  (98, 287, 1059, 1084, 1076, 1326, 1040, 110, 316, 134, 1047, 1043, 1056, 1071, 144, 1041, 1053, 145, 300,
-   76, 151, 1062, 1046, 102, 1042, 285),
-  (), (308, 2050, 1074, 99, 1072, 1060, 149, 2049, 157, 1052), (1063,), (), (1079, 1069, 1086, 284, 1078),
-  (1073, 1077, 1075), (), (1087, 2051, 1054), (1085,)),
- ((129, 71, 68, 137, 135, 132), (1057, 1047, 141, 535, 73, 67), (72, 134, 65, 1044, 1065, 66, 553, 801),
-  (1060, 1045, 1049, 292, 128, 537, 1063, 1043), (1064, 533, 275, 131),
-  (279, 74, 103, 1041, 105, 273, 147, 807, 548, 531, 1069, 145, 1046, 1125, 1075, 1050, 2048, 1058, 1051,
-   1067, 1048, 563, 1168, 1079, 1066, 2053, 106, 1056, 155, 1055, 2054, 301, 1073, 98, 1042, 1062, 530, 102),
-  (), (1059,), (1080, 1071, 1054), (1580, 1084, 1083, 1082, 1081, 1072, 1077, 1053, 557, 111, 414, 2055),
-  (1070,), (1076, 1074, 1078, 1085), (), (1086, 1087, 1052), ()),
- ((128, 70, 136, 68), (75, 1302, 138, 77, 74, 534, 1064, 139, 1044, 104, 143, 552, 1040, 148, 528),
-  (1051, 1067, 72, 555, 1053, 134, 276, 150, 1066, 285, 78, 539, 1047), (1065, 279, 554), (1076, 1057),
-  (1592, 106, 1050, 289, 151, 1071, 157, 79, 1058, 2048, 303, 155, 1062, 559, 1063, 1054, 1048, 144, 1041,
-   1049, 2053, 2054, 105, 1173, 1061, 1060, 542, 1082, 286),
-  (308,), (1043,), (1042, 1085, 1059, 1055, 1081, 573, 1075, 97, 1070, 1083, 2055, 1056),
-  (110, 159, 1072, 1074, 1079), (), (1073, 1078, 1077), (), (1086, 1052, 1084, 1068), (1069, 1087)),
- ((131, 64, 130, 67),
-  (128, 1040, 133, 76, 272, 65, 1058, 1059, 142, 1056, 99, 134, 98, 1046, 66, 141, 2048, 132, 79, 290, 1061,
-   1041),
-  (1052, 273), (293,), (1070, 156, 135), (101, 96, 1042, 1074, 1053, 140, 302, 291, 1043, 69, 1084, 1057),
-  (1071, 150, 1044, 110, 306, 1047), (1060, 1062, 2050, 284, 97, 2049, 151), (1045, 1075, 1063), (),
-  (1077, 1072, 1069, 157, 111, 316), (2051, 1055, 1079, 1078, 1073, 1076), (), (),
-  (1068, 1054, 1087, 1085, 1086)))
+PLANS = (((128, 70, 131, 69), (194, 143, 76, 2048, 1315, 1045, 67, 135), (142, 65),
+  (1046, 134, 1314, 1043, 98, 1071, 149, 1042, 99, 303, 1056), (406, 78),
+  (1052, 1063, 1041, 1134, 156, 1060, 1044, 273, 1040, 275, 1057, 133),
+  (111, 144, 1062, 1330, 1047, 103, 79, 1333), (2049, 140, 2050), (1054, 1084, 141, 1061, 1078, 77, 1075), (),
+  (1079, 1073, 1342), (1076, 1068, 1072), (), (1085, 1053, 2051, 1087, 1069, 1055), ()),
+ ((132, 64, 68, 202, 139), (), (1060, 71, 141, 66, 548, 135, 1040, 140, 272, 69, 292, 73, 1300, 532),
+  (1066, 1579, 1057, 1048, 1559, 554, 528, 1069, 353, 152, 134),
+  (1045, 1058, 279, 109, 136, 1080, 148, 568, 106, 1071),
+  (1049, 1061, 1050, 1063, 1132, 78, 1062, 1051, 1073, 2048, 556, 1046, 1065, 305, 557, 105, 561, 155, 2053),
+  (1064, 2054, 151, 76), (77, 1076, 1056, 1043), (1085, 147, 1041, 308, 1059, 1042), (1082,), (1083, 317),
+  (1054, 1084, 1081, 559, 142, 1077, 1079, 1075, 1078, 1074, 1072, 2055), (), (),
+  (1053, 1087, 1052, 1070, 1055, 1086)),
+ ((72, 129, 74, 133, 75, 137, 1048, 69, 1057, 65, 135, 536, 134, 801),
+  (1050, 1051, 1061, 73, 1065, 805, 131, 553, 539, 1056, 79, 1045, 142, 277), (136, 155, 1297, 1044, 1062),
+  (1060, 102, 544, 1049, 1063, 96, 153, 2048, 276, 292), (100,),
+  (1047, 1067, 1070, 2053, 1066, 1055, 1042, 1064, 110, 1046, 2054),
+  (1083, 302, 1059, 106, 1040, 99, 1058, 159), (1078, 1072, 566, 1076, 287, 1080, 308, 1043, 149), (560,),
+  (1087,), (1069, 543, 1082, 109),
+  (1081, 1052, 1086, 1074, 1077, 2055, 1068, 156, 575, 1079, 300, 1053, 1075, 1073), (), (1085,),
+  (1054, 1071, 1084)),
+ ((66, 70, 128, 130), (199, 143, 131, 1056, 1042, 288, 67, 76, 146, 77, 2048, 1058, 141, 1046, 1047),
+  (64, 274, 278, 1057, 290), (1043,), (150, 151, 134, 1061, 1063, 275, 78, 1059, 1074),
+  (97, 306, 99, 1180, 1045, 284, 1040, 1053, 101, 144, 1041),
+  (1135, 1079, 2049, 311, 1054, 1060, 1078, 158, 285, 286), (2050,), (157, 1062, 1044, 1073, 1075), (),
+  (1072, 1077), (1076, 1086, 1070), (), (2051,), (1084, 1085, 1055, 1069, 1068, 1087)))
 
 
 def split_kernel(
@@ -772,16 +772,22 @@
         return pl.ds(start if isinstance(start, int) else pl.multiple_of(start, head_size), count)
 
     def project(unit, buffer, slot):
-        keys = stack(
-            [wbuf.at[relation, rows_of(head * head_rows + head_size, 2 * head_size), :] for relation, head in unit]
-        )
+        straight, turned = [], []
+        for relation, head in unit:
+            start = head * head_rows + head_size
+            straight.append(wbuf[relation, rows_of(start, 2 * head_size), :])
+            for offset, count in ((half_rows, half_rows), (0, half_rows), (head_size, head_size)):
+                place = start + offset
+                place = place if isinstance(place, int) else pl.multiple_of(place, half_rows)
+                turned.append(wbuf[relation, pl.ds(place, count), :])
+        keys = jnp.concatenate(straight + turned, axis=0)
 
         def step_of(step, carry):
             rows = pl.ds(pl.multiple_of(step * span, 16), span)
             made = lax.dot_general(normed[slot, rows, :], keys, transposed, preferred_element_type=f32)
             for head in range(2):
-                block = made[:, head * LANES : (head + 1) * LANES]
-                block = jnp.where(low, rotate(block, cos[rows, :], sin[rows, :]), block)
+                block = made[:, head * LANES : (head + 1) * LANES] * cos[rows, :]
+                block += made[:, (head + 2) * LANES : (head + 3) * LANES] * sin[rows, :]
                 pbuf[buffer, slot, rows, head * LANES : (head + 1) * LANES] = block.astype(bf16)
             return carry
 
@@ -1008,8 +1014,8 @@
         weight,
         out_weight,
         dense_weight,
-        jnp.asarray(cosine),
-        jnp.asarray(sine),
+        jnp.asarray(np.where(np.arange(LANES) < head_size, cosine, np.float32(1))),
+        jnp.asarray(np.where(np.arange(LANES) < head_size, sine, np.float32(0))),
         jnp.asarray(split),
     )
 

time: 45.6 us -> 44.3 us (0.971)
  Pallas kernels: 44.2 us -> 42.9 us
    pallas_call x1, Pallas kernels: 44.2 us -> 42.9 us  [split_call(): pl.pallas_call(functools.partial(split_kernel, (n_dp, n_mp, head_size)),...]
where the time goes in v5:
time: 44.3 us; the launch traced here: 44.2 us
  Pallas kernels  42.9 us (97%)
  local copies, waits for them, and re-layouts  1.26 us (3%)
    pallas_call x1, Pallas kernels, split_call(): pl.pallas_call(functools.partial(split_kernel, (n_dp, n_mp, head_size)),...  42.9 us
    unnamed x1, local copies, waits for them, and re-layouts  1.26 us

profile of v5, /device:TPU:0, one launch (start us, length us, event | category | flops | bytes accessed | tf_op | source)
XLA Modules:
  0.0 44.2 jit_solution(5833904939362819630)
XLA Ops:
  0.0 42.9 %score_split.1 = f32[4,16]{1,0:T(4,128)} custom-call(s32[32]{0:T(128)} %sequence_hbm.1, s32[24]{0:T(128)} %lengths_hbm.1, s32[32,64]{1,0:T(8,128)} %codes_hbm.1, s32[24,640]{1,0:T(8,128)} %tokens_hbm.1, s32[1,32]{1,0:T(1,128)} %bitcast.10, f32[1280]{0:T(1024)} %gain_hbm.1, f32[1280]{0:T(1024)} %final_gain_hbm.1, bf16[33,1280]{1,0:T(8,128)(2,1)} %bitcast.9, ...), custom_call_target="tpu_custom_call" | custom-call | tf_op jit(solution)/shard_map/score_split/pallas_call | solution.py:975
  42.9 1.3 %copy.18 = f32[4,16]{1,0:T(4,128)} copy(f32[4,16]{1,0:T(4,128)} %score_split.1) | data formatting | bytes 512

commit v6 on v5

--- a/solution.py
+++ b/solution.py
@@ -545,19 +545,19 @@
     def signal(semaphore, target):
         pl.semaphore_signal(semaphore, inc=1, device_id=target, device_id_type=MESH)
 
-    for link in "dxye":
-        signal(barrier, where[link])
-
-    @pl.when(middle)
-    def _():
-        signal(barrier, where["m"])
-
     def local(index, source, target):
         copy = pltpu.make_async_copy(source, target, local_sem.at[index])
         copy.start()
         return copy
 
     weight_copy = local(1, weight_hbm.at[core], wbuf.at[0])
+    for link in "dxye":
+        signal(barrier, where[link])
+
+    @pl.when(middle)
+    def _():
+        signal(barrier, where["m"])
+
     hidden_copy = local(0, hidden_hbm, hidden)
     small_copies = [
         local(7 + place, source, target)
@@ -887,20 +887,33 @@
     attend_both(3, across, 1)
     tokens_step(5)
     service(14)
-    mix(1, firsts, seconds, across)
-    inbox_copy = pltpu.make_async_remote_copy(
-        src_ref=mixed.at[pl.ds(masks, masks), :],
-        dst_ref=inbox,
-        send_sem=swap_send_sem.at[3],
-        recv_sem=swap_sem.at[3],
-        device_id=(partner, mp),
-        device_id_type=MESH,
-    )
-    inbox_copy.start()
+    out_weights = [
+        obuf.at[relation, rows_of(head * head_size, head_size), :]
+        for unit in (firsts, seconds, across)
+        for relation, head in unit
+    ]
+
+    def inbox_copy(part):
+        lanes = pl.ds(part * (feature // 2), feature // 2)
+        return pltpu.make_async_remote_copy(
+            src_ref=mixed.at[pl.ds(masks, masks), lanes],
+            dst_ref=inbox.at[:, lanes],
+            send_sem=swap_send_sem.at[3 + part],
+            recv_sem=swap_sem.at[3 + part],
+            device_id=(partner, mp),
+            device_id_type=MESH,
+        )
+
+    for part in range(2):
+        lanes = slice(part * (feature // 2), (part + 1) * (feature // 2))
+        weights = jnp.concatenate([ref[:, lanes] for ref in out_weights], axis=0)
+        mixed[:, lanes] += jnp.dot(context[:, LANES:], weights, preferred_element_type=f32)
+        inbox_copy(part).start()
     dense_copy.wait()
     for copy in late_copies:
         copy.wait()
-    inbox_copy.wait_recv()
+    inbox_copy(0).wait_recv()
+    inbox_copy(1).wait_recv()
     residual = mixed[:masks, :] + inbox[...]
     normed_final = (layer_norm(residual) * final_gain_ref[...].reshape(1, feature)).astype(bf16)
     dense_out = jnp.dot(normed_final, dense[...], preferred_element_type=f32)
@@ -927,7 +940,8 @@
 
     for step in reversed(range(1, devices)):
         score_copy(step).start()
-    inbox_copy.wait_send()
+    inbox_copy(0).wait_send()
+    inbox_copy(1).wait_send()
     norm_copy.wait_send()
     rows_copy(0, 1, "d", 0).wait_send()
 
@@ -1002,8 +1016,8 @@
             dma((n_mp - 1, 16)),
             dma((2, n_mp - 1)),
             dma((2,)),
-            dma((4,)),
-            dma((4,)),
+            dma((5,)),
+            dma((5,)),
             dma((2,)),
             pltpu.SemaphoreType.REGULAR((5,)),
         ],

time: 44.3 us -> 44.3 us (level)
  no operation moved by 1% of the time
where the time goes in v6:
time: 44.3 us; the launch traced here: 44.1 us
  Pallas kernels  42.9 us (97%)
  local copies, waits for them, and re-layouts  1.26 us (3%)
    pallas_call x1, Pallas kernels, split_call(): pl.pallas_call(functools.partial(split_kernel, (n_dp, n_mp, head_size)),...  42.9 us
    unnamed x1, local copies, waits for them, and re-layouts  1.26 us

profile of v6, /device:TPU:0, one launch (start us, length us, event | category | flops | bytes accessed | tf_op | source)
XLA Modules:
  0.0 44.1 jit_solution(17687933029191911175)
XLA Ops:
  0.0 42.9 %score_split.1 = f32[4,16]{1,0:T(4,128)} custom-call(s32[32]{0:T(128)} %sequence_hbm.1, s32[24]{0:T(128)} %lengths_hbm.1, s32[32,64]{1,0:T(8,128)} %codes_hbm.1, s32[24,640]{1,0:T(8,128)} %tokens_hbm.1, s32[1,32]{1,0:T(1,128)} %bitcast.10, f32[1280]{0:T(1024)} %gain_hbm.1, f32[1280]{0:T(1024)} %final_gain_hbm.1, bf16[33,1280]{1,0:T(8,128)(2,1)} %bitcast.9, ...), custom_call_target="tpu_custom_call" | custom-call | tf_op jit(solution)/shard_map/score_split/pallas_call | solution.py:989
  42.9 1.3 %copy.18 = f32[4,16]{1,0:T(4,128)} copy(f32[4,16]{1,0:T(4,128)} %score_split.1) | data formatting | bytes 512
